TPU v7x, 32 devices: a whole 2x2x4 slice. The times are simulated.
32 devices in a mesh: gx: 4 (over x, core), gy: 8 (over z, y).
Axes of the slice: x: 2, y: 2, z: 4, core: 2. Of those that a mesh axis runs over, the one named last changes fastest.
Arguments:
- fine_start: float32 [3, 1024, 4096], P(None, 'gx', 'gy'), may hold values from -6 to 6
- fine_known: float32 [3, 1024, 4096], P(None, 'gx', 'gy'), may hold values from -18 to 18
- fine_mu: float32 [1024, 4096], P('gx', 'gy'), may hold values from 1 to 10
- coarse_start: float32 [3, 512, 2048], P(None, ('gx', 'gy')), may hold values from -6 to 6
- coarse_known: float32 [3, 512, 2048], P(None, ('gx', 'gy')), may hold values from -18 to 18
- coarse_mu: float32 [512, 2048], P(('gx', 'gy')), may hold values from 1 to 10
Outputs:
- fine_ghost: float32 [3, 1024, 4096], P(None, 'gx', 'gy')
- coarse_ghost: float32 [3, 512, 2048], P(None, ('gx', 'gy'))
- norms: float32 [3], replicated
All inputs are finite; a program needn't handle non-finite values.
Results may differ from a plain program's by a relative error of at most 0.0001.
Values sent between devices are 32-bit elements; how exact they have to be, the bound alone decides.
A program may use at most 128 MiB of HBM per device.

v0:
```python
import functools

import jax
import jax.numpy as jnp
from jax import lax
from jax.experimental import pallas as pl
from jax.experimental.pallas import tpu as pltpu
from jax.sharding import PartitionSpec as P

ITERS = 3
LANES = 128
SUB = 8
UNROLL = 2
MESH = pl.DeviceIdType.MESH
DIRECTIONS = ((-1, 0), (1, 0), (0, -1), (0, 1), (-1, -1), (1, 1), (-1, 1), (1, -1))


def lane_index():
    return lax.broadcasted_iota(jnp.int32, (SUB, LANES), 1)


def roll_lanes(cells, shift):
    shift = shift % LANES
    return cells if shift == 0 else pltpu.roll(cells, shift, 1)


def from_left(halves, halo):
    first = lane_index() == 0
    rolled = [roll_lanes(cells, 1) for cells in halves]
    return [jnp.where(first, before, own) for before, own in zip([halo] + rolled[:-1], rolled)]


def from_right(halves, halo):
    last = lane_index() == LANES - 1
    rolled = [roll_lanes(cells, LANES - 1) for cells in halves]
    return [jnp.where(last, after, own) for own, after in zip(rolled, rolled[1:] + [halo])]


def kernel(
    n_gx,
    n_gy,
    cells_total,
    fine_start,
    fine_known,
    fine_mu,
    coarse_start,
    coarse_known,
    coarse_mu,
    fine_out,
    coarse_out,
    norms_out,
    raw_start,
    raw_known,
    raw_mu,
    fine_a,
    fine_b,
    known,
    diag,
    inverse,
    patch_start,
    patch_known,
    patch_mu,
    coarse_a,
    coarse_b,
    patch_out,
    fine_row_send,
    fine_row_recv,
    fine_col_send,
    fine_col_recv,
    row_send,
    row_recv,
    col_send,
    col_recv,
    corner_recv,
    packed,
    fine_halo,
    coarse_halo,
    norm_x,
    norm_y,
    load_sem,
    store_sem,
    own_sem,
    move_send,
    move_recv,
    fine_send,
    fine_recv,
    halo_send,
    halo_recv,
    back_own,
    back_send,
    back_recv,
    normx_send,
    normx_recv,
    normy_send,
    normy_recv,
):
    gx = lax.axis_index("gx")
    gy = lax.axis_index("gy")
    fine, coarse = (fine_a, fine_b), (coarse_a, coarse_b)
    comps, rows, width = patch_start.shape
    halves = width // LANES
    blocks = rows // SUB
    own_rows = coarse_start.shape[1]
    lane = lane_index()

    loads = []
    for which, (source, target) in enumerate(
        ((fine_start, raw_start), (fine_mu, raw_mu), (fine_known, raw_known))
    ):
        for tile in range(2 * halves):
            at = pl.ds(tile * LANES, LANES)
            view = source.at[:, at] if len(source.shape) == 2 else source.at[:, :, at]
            loads.append(
                pltpu.make_async_copy(view, target.at[tile], load_sem.at[which, tile])
            )
    for copy in loads:
        copy.start()

    for ref in (fine_row_recv, fine_col_recv, row_recv, col_recv, corner_recv, row_send, fine_row_send):
        ref[...] = jnp.zeros_like(ref)

    barrier = pltpu.get_barrier_semaphore()

    def greet_gy(step, carry):
        pl.semaphore_signal(
            barrier, inc=1, device_id={"gy": lax.rem(gy + step, n_gy)}, device_id_type=MESH
        )
        return carry

    def greet_gx(step, carry):
        pl.semaphore_signal(
            barrier, inc=1, device_id={"gx": lax.rem(gx + step, n_gx)}, device_id_type=MESH
        )
        return carry

    lax.fori_loop(1, n_gy, greet_gy, 0)
    lax.fori_loop(1, n_gx, greet_gx, 0)

    def inside(direction):
        dx, dy = DIRECTIONS[direction]
        checks = []
        if dx:
            checks.append(gx > 0 if dx < 0 else gx < n_gx - 1)
        if dy:
            checks.append(gy > 0 if dy < 0 else gy < n_gy - 1)
        return functools.reduce(jnp.logical_and, checks)

    for direction in range(4, 8):
        dx, dy = DIRECTIONS[direction]

        @pl.when(inside(direction))
        def _():
            pl.semaphore_signal(
                barrier, inc=1, device_id={"gx": gx + dx, "gy": gy + dy}, device_id_type=MESH
            )

    sides_x = (gx > 0).astype(jnp.int32) + (gx < n_gx - 1).astype(jnp.int32)
    sides_y = (gy > 0).astype(jnp.int32) + (gy < n_gy - 1).astype(jnp.int32)
    pl.semaphore_wait(barrier, n_gy - 1 + n_gx - 1 + sides_x * sides_y)

    moved = ((coarse_start, patch_start), (coarse_known, patch_known), (coarse_mu, patch_mu))

    def move(which, owner, place, sem):
        source, target = moved[which]
        columns = pl.ds(pl.multiple_of(owner * width, LANES), width)
        lines = pl.ds(pl.multiple_of(place * own_rows, SUB), own_rows)
        if len(source.shape) == 2:
            return source.at[:, columns], target.at[lines, :]
        return source.at[:, :, columns], target.at[:, lines, :]

    def own_move(which):
        source, target = move(which, gy, gy, None)
        return pltpu.make_async_copy(source, target, own_sem.at[which])

    def peer_move(which, step):
        peer = lax.rem(gy + step, n_gy)
        source, target = move(which, peer, gy, None)
        return pltpu.make_async_remote_copy(
            source,
            target,
            move_send.at[which, step],
            move_recv.at[which, step],
            device_id={"gy": peer},
            device_id_type=MESH,
        )

    def wait_moves(which):
        own_move(which).wait()

        def body(step, carry):
            peer = lax.rem(gy + n_gy - step, n_gy)
            source, target = move(which, gy, peer, None)
            pltpu.make_async_remote_copy(
                source,
                target,
                move_send.at[which, step],
                move_recv.at[which, step],
                device_id={"gy": lax.rem(gy + step, n_gy)},
                device_id_type=MESH,
            ).wait()
            return carry

        lax.fori_loop(1, n_gy, body, 0)

    def send_moves(which):
        def body(step, carry):
            peer_move(which, step).start()
            return carry

        lax.fori_loop(1, n_gy, body, 0)
        own_move(which).start()

    send_moves(0)

    half_lane = lane < LANES // 2
    evens_first = jnp.where(half_lane, 2 * lane, 2 * lane - LANES + 1)
    odds_first = jnp.where(half_lane, 2 * lane + 1, 2 * lane - LANES)

    def split_columns(a, b):
        a = jnp.take_along_axis(a, evens_first, axis=1)
        b = jnp.take_along_axis(b, odds_first, axis=1)
        return (
            jnp.where(half_lane, a, b),
            pltpu.roll(jnp.where(half_lane, b, a), LANES // 2, 1),
        )

    def split_field(raw, put):
        def body(block, carry):
            out = []
            for comp in range(comps):
                for parity in range(2):
                    for half in range(halves):
                        at = pl.ds(block * 2 * SUB + parity, SUB, stride=2)
                        both = split_columns(
                            raw[2 * half, comp, at, :], raw[2 * half + 1, comp, at, :]
                        )
                        out.append((comp, parity, half, both))
            for comp, parity, half, both in out:
                put(comp, parity, 0, half, block, both[0])
                put(comp, parity, 1, half, block, both[1])
            return carry

        lax.fori_loop(0, blocks, body, 0)

    def rows_of(block, shift=0):
        if shift == 0:
            return pl.ds(pl.multiple_of(block * SUB + SUB, SUB), SUB)
        return pl.ds(block * SUB + SUB + shift, SUB)

    def plain(block):
        return pl.ds(pl.multiple_of(block * SUB, SUB), SUB)

    def put_start(comp, parity, side, half, block, cells):
        fine[0][comp, parity, side, half, rows_of(block), :] = cells

    def put_known(comp, parity, side, half, block, cells):
        known[comp, parity, side, half, plain(block), :] = cells

    def split_mu(block, carry):
        out = []
        for parity in range(2):
            for half in range(halves):
                at = pl.ds(block * 2 * SUB + parity, SUB, stride=2)
                both = split_columns(raw_mu[2 * half, at, :], raw_mu[2 * half + 1, at, :])
                for side in range(2):
                    total = both[side] + 1.0
                    out.append((parity, side, half, total, 1.0 / total))
        for parity, side, half, total, reciprocal in out:
            diag[parity, side, half, plain(block), :] = total
            inverse[parity, side, half, plain(block), :] = reciprocal
        return carry

    def place_start(block, carry):
        for comp in range(comps):
            for half in range(halves):
                coarse[0][comp, half, rows_of(block), :] = patch_start[
                    comp, plain(block), half * LANES : (half + 1) * LANES
                ]
        return carry

    def pack(edges, target):
        def body(block, carry):
            out = []
            for way, at in ((0, 0), (1, LANES - 1)):
                for k, edge in enumerate(edges(way, block)):
                    out.append((SUB * way + k, roll_lanes(edge, SUB * way + k - at)))
            cells = jnp.zeros((SUB, LANES), jnp.float32)
            for k, edge in out:
                cells = jnp.where(lane == k, edge, cells)
            packed[plain(block), :] = cells
            return carry

        lax.fori_loop(0, blocks, body, 0, unroll=4)
        target[...] = packed[...].T[: 2 * SUB]

    def message(rows_out, rows_in, cols_out, cols_in, sends, recvs, sweep, direction):
        dx, dy = DIRECTIONS[direction]
        way = direction % 2
        if direction < 2:
            source, target = rows_out.at[sweep, way], rows_in.at[sweep, 1 - way]
        elif direction < 4:
            source = cols_out.at[sweep, pl.ds(SUB * way, SUB), :]
            target = cols_in.at[sweep, pl.ds(SUB * (1 - way), SUB), :]
        else:
            half = 0 if dy < 0 else halves - 1
            source = rows_out.at[sweep, 0 if dx < 0 else 1, half]
            target = corner_recv.at[sweep, (direction ^ 1) - 4]
        return pltpu.make_async_remote_copy(
            source,
            target,
            sends.at[sweep, direction],
            recvs.at[sweep, direction ^ 1],
            device_id={"gx": gx + dx, "gy": gy + dy},
            device_id_type=MESH,
        )

    fine_message = functools.partial(
        message, fine_row_send, fine_row_recv, fine_col_send, fine_col_recv, fine_send, fine_recv
    )
    coarse_message = functools.partial(
        message, row_send, row_recv, col_send, col_recv, halo_send, halo_recv
    )

    def start_all(of, sweep, directions):
        for direction in directions:

            @pl.when(inside(direction))
            def _():
                of(sweep, direction).start()

    def wait_all(of, sweep, directions):
        for direction in directions:

            @pl.when(inside(direction))
            def _():
                of(sweep, direction).wait_send()
                of(sweep, direction ^ 1).wait_recv()

    def send_fine(sweep):
        buf = sweep % 2
        for way, line in enumerate((SUB, SUB + rows - 1)):
            for half in range(halves):
                for comp in range(comps):
                    for side in range(2):
                        at = 2 * comp + side
                        fine_row_send[sweep, way, half, at : at + 1, :] = fine[buf][
                            comp, way, side, half, line : line + 1, :
                        ]
        start_all(fine_message, sweep, (0, 1))

        def edges(way, block):
            half = way * (halves - 1)
            return [
                fine[buf][k // 2, k % 2, way, half, rows_of(block), :] for k in range(2 * comps)
            ]

        pack(edges, fine_col_send.at[sweep])
        start_all(fine_message, sweep, (2, 3))

    def take_fine(sweep):
        buf = sweep % 2
        wait_all(fine_message, sweep, range(4))
        for half in range(halves):
            for comp in range(comps):
                for side in range(2):
                    at = 2 * comp + side
                    fine[buf][comp, 1, side, half, SUB - 1 : SUB, :] = fine_row_recv[
                        sweep, 0, half, at : at + 1, :
                    ]
                    fine[buf][comp, 0, side, half, SUB + rows : SUB + rows + 1, :] = (
                        fine_row_recv[sweep, 1, half, at : at + 1, :]
                    )
        fine_halo[SUB : SUB + rows, :] = fine_col_recv[sweep].T

    def send_coarse(sweep):
        buf = sweep % 2
        for way, line in enumerate((SUB, SUB + rows - 1)):
            for half in range(halves):
                for comp in range(comps):
                    row_send[sweep, way, half, comp : comp + 1, :] = coarse[buf][
                        comp, half, line : line + 1, :
                    ]
        start_all(coarse_message, sweep, (4, 5, 6, 7, 0, 1))

        def edges(way, block):
            half = way * (halves - 1)
            return [coarse[buf][k, half, rows_of(block), :] for k in range(comps)]

        pack(edges, col_send.at[sweep])
        start_all(coarse_message, sweep, (2, 3))

    def take_coarse(sweep):
        buf = sweep % 2
        wait_all(coarse_message, sweep, range(8))
        for half in range(halves):
            for comp in range(comps):
                for way, line in enumerate((SUB - 1, SUB + rows)):
                    coarse[buf][comp, half, line : line + 1, :] = row_recv[
                        sweep, way, half, comp : comp + 1, :
                    ]
        coarse_halo[SUB : SUB + rows, :] = col_recv[sweep].T
        corner_lanes = ((0, 2), (3, 1))
        for corners, line in zip(corner_lanes, (SUB - 1, SUB + rows)):
            held = jnp.zeros((SUB, LANES), jnp.float32)
            for way, corner in enumerate(corners):
                block = corner_recv[sweep, corner]
                for comp in range(comps):
                    k = SUB * way + comp
                    lifted = pltpu.roll(block, SUB - comp, 0) if comp else block
                    moved = roll_lanes(lifted, k - (0 if way else LANES - 1))
                    held = jnp.where(lane == k, moved, held)
            coarse_halo[line : line + 1, :] = held[0:1, :]

    def halo_pair(halo, k, lines):
        cells = halo[lines, :]
        return roll_lanes(cells, -k), roll_lanes(cells, LANES - 1 - SUB - k)

    def coarse_pass(buf, last):
        def body(block, totals):
            totals = list(totals)
            lines = plain(block)
            out = []
            scales = [
                patch_mu[lines, half * LANES : (half + 1) * LANES] + 1.0 for half in range(halves)
            ]
            reciprocals = [1.0 / scale for scale in scales]
            for comp in range(comps):
                left, right = halo_pair(coarse_halo, comp, rows_of(block))
                own = [coarse[buf][comp, half, rows_of(block), :] for half in range(halves)]
                lefts, rights = from_left(own, left), from_right(own, right)
                for half in range(halves):
                    columns = slice(half * LANES, (half + 1) * LANES)
                    near = (
                        coarse[buf][comp, half, rows_of(block, 1), :]
                        + coarse[buf][comp, half, rows_of(block, -1), :]
                        + rights[half]
                        + lefts[half]
                    )
                    below = (
                        fine[buf][comp, 0, 0, half, rows_of(block), :]
                        + fine[buf][comp, 1, 0, half, rows_of(block), :]
                        + fine[buf][comp, 0, 1, half, rows_of(block), :]
                        + fine[buf][comp, 1, 1, half, rows_of(block), :]
                    )
                    res = (
                        patch_known[comp, lines, columns]
                        + 0.25 * near
                        + 0.125 * below
                        - scales[half] * own[half]
                    )
                    totals[comp] = totals[comp] + res * res
                    out.append((comp, half, own[half] + res * reciprocals[half]))
            for comp, half, new in out:
                if last:
                    patch_out[comp, lines, half * LANES : (half + 1) * LANES] = new
                else:
                    coarse[1 - buf][comp, half, rows_of(block), :] = new
            return tuple(totals)

        zero = jnp.zeros((SUB, LANES), jnp.float32)
        return sum(lax.fori_loop(0, blocks, body, (zero,) * comps, unroll=UNROLL))

    def fine_pass(buf):
        def body(block, totals):
            totals = list(totals)
            out = []
            for comp in range(comps):
                mid = [coarse[buf][comp, half, rows_of(block), :] for half in range(halves)]
                mid_left, mid_right = halo_pair(coarse_halo, comp, rows_of(block))
                for parity in range(2):
                    shift = 1 if parity else -1
                    far_left, far_right = halo_pair(coarse_halo, comp, rows_of(block, shift))
                    line = [
                        0.75 * mid[half]
                        + 0.25 * coarse[buf][comp, half, rows_of(block, shift), :]
                        for half in range(halves)
                    ]
                    line_left = from_left(line, 0.75 * mid_left + 0.25 * far_left)
                    line_right = from_right(line, 0.75 * mid_right + 0.25 * far_right)
                    fine_left, fine_right = halo_pair(fine_halo, 2 * comp + parity, rows_of(block))
                    evens, odds = (
                        [fine[buf][comp, parity, side, half, rows_of(block), :] for half in range(halves)]
                        for side in range(2)
                    )
                    before, after = from_left(odds, fine_left), from_right(evens, fine_right)
                    for half in range(halves):
                        for side in range(2):
                            own = odds[half] if side else evens[half]
                            lateral = (
                                evens[half] + after[half] if side else odds[half] + before[half]
                            )
                            near = (
                                fine[buf][comp, 1 - parity, side, half, rows_of(block), :]
                                + fine[buf][comp, 1 - parity, side, half, rows_of(block, shift), :]
                                + lateral
                            )
                            spread = 0.75 * line[half] + 0.25 * (
                                line_right[half] if side else line_left[half]
                            )
                            res = (
                                known[comp, parity, side, half, plain(block), :]
                                + 0.25 * near
                                + 0.5 * spread
                                - diag[parity, side, half, plain(block), :] * own
                            )
                            totals[comp] = totals[comp] + res * res
                            new = own + res * inverse[parity, side, half, plain(block), :]
                            out.append((comp, parity, side, half, new))
            for comp, parity, side, half, new in out:
                fine[1 - buf][comp, parity, side, half, rows_of(block), :] = new
            return tuple(totals)

        zero = jnp.zeros((SUB, LANES), jnp.float32)
        return sum(lax.fori_loop(0, blocks, body, (zero,) * comps))

    def back_place(owner, place):
        return (
            patch_out.at[:, pl.ds(pl.multiple_of(owner * own_rows, SUB), own_rows), :],
            coarse_out.at[:, :, pl.ds(pl.multiple_of(place * width, LANES), width)],
        )

    def back_move(step, place_step):
        peer = lax.rem(gy + step, n_gy)
        source, _ = back_place(peer, gy)
        _, target = back_place(peer, lax.rem(gy + place_step, n_gy))
        return pltpu.make_async_remote_copy(
            source,
            target,
            back_send.at[step],
            back_recv.at[step],
            device_id={"gy": peer},
            device_id_type=MESH,
        )

    def back_start(step, carry):
        back_move(step, 0).start()
        return carry

    def back_wait(step, carry):
        back_move(step, n_gy - step).wait()
        return carry

    own_back = pltpu.make_async_copy(*back_place(gy, gy), back_own.at[0])
    row = lax.broadcasted_iota(jnp.int32, (SUB, LANES), 0)
    totals = [None] * ITERS
    tiles = 2 * halves
    for copy in loads[:tiles]:
        copy.wait()
    split_field(raw_start, put_start)
    send_fine(0)
    send_moves(2)
    for copy in loads[tiles : 2 * tiles]:
        copy.wait()
    lax.fori_loop(0, blocks, split_mu, 0, unroll=2)
    for copy in loads[2 * tiles :]:
        copy.wait()
    split_field(raw_known, put_known)
    wait_moves(0)
    lax.fori_loop(0, blocks, place_start, 0, unroll=4)
    send_coarse(0)
    send_moves(1)
    take_fine(0)
    take_coarse(0)

    totals[0] = fine_pass(0)
    send_fine(1)
    wait_moves(2)
    wait_moves(1)
    totals[0] = totals[0] + coarse_pass(0, False)
    for sweep in range(1, ITERS):
        buf = sweep % 2
        last = sweep == ITERS - 1
        if sweep == 1:
            send_coarse(1)
        take_coarse(sweep)
        totals[sweep] = coarse_pass(buf, last)
        if last:
            lax.fori_loop(1, n_gy, back_start, 0)
            own_back.start()
        else:
            send_coarse(sweep + 1)
        take_fine(sweep)
        totals[sweep] = totals[sweep] + fine_pass(buf)
        if not last:
            send_fine(sweep + 1)
    sums = jnp.zeros((SUB, LANES), jnp.float32)
    for sweep in range(ITERS):
        sums = jnp.where(row == sweep, jnp.sum(totals[sweep], axis=0, keepdims=True), sums)

    def spread_sum(slots, axis, me, count, send_sems, recv_sems, between):
        def message(step, place_step):
            peer = lax.rem(me + step, count)
            return pltpu.make_async_remote_copy(
                slots.at[me],
                slots.at[lax.rem(me + place_step, count)],
                send_sems.at[step],
                recv_sems.at[step],
                device_id={axis: peer},
                device_id_type=MESH,
            )

        def start(step, carry):
            message(step, 0).start()
            return carry

        def wait(step, carry):
            message(step, count - step).wait()
            return carry

        lax.fori_loop(1, count, start, 0)
        between()
        lax.fori_loop(1, count, wait, 0)
        return lax.fori_loop(
            0, count, lambda i, acc: acc + slots[i], jnp.zeros((SUB, LANES), jnp.float32)
        )

    final = ITERS % 2
    weave_a = jnp.where(lane % 2 == 0, lane // 2, lane // 2 + LANES // 2)
    weave_b = jnp.where(lane % 2 == 0, lane // 2 + LANES // 2, lane // 2)

    def weave(block, carry):
        out = []
        for comp in range(comps):
            for parity in range(2):
                for half in range(halves):
                    even = fine[final][comp, parity, 0, half, rows_of(block), :]
                    odd = fine[final][comp, parity, 1, half, rows_of(block), :]
                    odd = pltpu.roll(odd, LANES // 2, 1)
                    at = pl.ds(block * 2 * SUB + parity, SUB, stride=2)
                    a = jnp.take_along_axis(jnp.where(half_lane, even, odd), weave_a, axis=1)
                    b = jnp.take_along_axis(jnp.where(half_lane, odd, even), weave_b, axis=1)
                    out.append((2 * half, comp, at, a))
                    out.append((2 * half + 1, comp, at, b))
        for tile, comp, at, cells in out:
            raw_start[tile, comp, at, :] = cells
        return carry

    stores = [
        pltpu.make_async_copy(
            raw_start.at[tile],
            fine_out.at[:, :, pl.ds(tile * LANES, LANES)],
            store_sem.at[tile],
        )
        for tile in range(tiles)
    ]

    def put_fine():
        lax.fori_loop(0, blocks, weave, 0)
        for copy in stores:
            copy.start()

    norm_x[gx] = sums
    partial = spread_sum(norm_x, "gx", gx, n_gx, normx_send, normx_recv, put_fine)
    norm_y[gy] = partial
    whole = spread_sum(norm_y, "gy", gy, n_gy, normy_send, normy_recv, lambda: None)
    root = jnp.sqrt(jnp.sum(whole, axis=1, keepdims=True) / cells_total)
    norms_out[...] = jnp.broadcast_to(root, norms_out.shape)

    for copy in stores:
        copy.wait()
    own_back.wait()
    lax.fori_loop(1, n_gy, back_wait, 0)


def on_device(n_gx, n_gy, fine_start, fine_known, fine_mu, coarse_start, coarse_known, coarse_mu):
    comps, fine_rows, fine_cols = fine_start.shape
    rows, width = fine_rows // 2, fine_cols // 2
    halves = width // LANES
    tiles = 2 * halves
    padded = rows + 2 * SUB
    cells_total = 3.0 * (fine_mu.size + coarse_mu.size) * n_gx * n_gy
    f32 = jnp.float32
    dma = pltpu.SemaphoreType.DMA
    anywhere = pl.BlockSpec(memory_space=pl.ANY)
    fine_ghost, coarse_ghost, norms = pl.pallas_call(
        functools.partial(kernel, n_gx, n_gy, cells_total),
        out_shape=(
            jax.ShapeDtypeStruct(fine_start.shape, f32),
            jax.ShapeDtypeStruct(coarse_start.shape, f32),
            jax.ShapeDtypeStruct((SUB, LANES), f32),
        ),
        in_specs=[pl.BlockSpec(memory_space=pltpu.HBM)] * 6,
        out_specs=(anywhere, anywhere, pl.BlockSpec(memory_space=pltpu.VMEM)),
        scratch_shapes=[
            pltpu.VMEM((tiles, comps, fine_rows, LANES), f32),
            pltpu.VMEM((tiles, comps, fine_rows, LANES), f32),
            pltpu.VMEM((tiles, fine_rows, LANES), f32),
            pltpu.VMEM((comps, 2, 2, halves, padded, LANES), f32),
            pltpu.VMEM((comps, 2, 2, halves, padded, LANES), f32),
            pltpu.VMEM((comps, 2, 2, halves, rows, LANES), f32),
            pltpu.VMEM((2, 2, halves, rows, LANES), f32),
            pltpu.VMEM((2, 2, halves, rows, LANES), f32),
            pltpu.VMEM((comps, rows, width), f32),
            pltpu.VMEM((comps, rows, width), f32),
            pltpu.VMEM((rows, width), f32),
            pltpu.VMEM((comps, halves, padded, LANES), f32),
            pltpu.VMEM((comps, halves, padded, LANES), f32),
            pltpu.VMEM((comps, rows, width), f32),
            pltpu.VMEM((ITERS, 2, halves, SUB, LANES), f32),
            pltpu.VMEM((ITERS, 2, halves, SUB, LANES), f32),
            pltpu.VMEM((ITERS, 2 * SUB, rows), f32),
            pltpu.VMEM((ITERS, LANES, rows), f32),
            pltpu.VMEM((ITERS, 2, halves, SUB, LANES), f32),
            pltpu.VMEM((ITERS, 2, halves, SUB, LANES), f32),
            pltpu.VMEM((ITERS, 2 * SUB, rows), f32),
            pltpu.VMEM((ITERS, LANES, rows), f32),
            pltpu.VMEM((ITERS, 4, SUB, LANES), f32),
            pltpu.VMEM((rows, LANES), f32),
            pltpu.VMEM((padded, LANES), f32),
            pltpu.VMEM((padded, LANES), f32),
            pltpu.VMEM((n_gx, SUB, LANES), f32),
            pltpu.VMEM((n_gy, SUB, LANES), f32),
            dma((3, tiles)),
            dma((tiles,)),
            dma((3,)),
            dma((3, n_gy)),
            dma((3, n_gy)),
            dma((ITERS, 4)),
            dma((ITERS, 4)),
            dma((ITERS, 8)),
            dma((ITERS, 8)),
            dma((1,)),
            dma((n_gy,)),
            dma((n_gy,)),
            dma((n_gx,)),
            dma((n_gx,)),
            dma((n_gy,)),
            dma((n_gy,)),
        ],
        compiler_params=pltpu.CompilerParams(
            collective_id=0, has_side_effects=True, vmem_limit_bytes=67043328
        ),
    )(fine_start, fine_known, fine_mu, coarse_start, coarse_known, coarse_mu)
    return fine_ghost, coarse_ghost, norms[:ITERS, 0]


def solution(mesh):
    n_gx, n_gy = mesh.shape["gx"], mesh.shape["gy"]
    return jax.shard_map(
        functools.partial(on_device, n_gx, n_gy),
        mesh=mesh,
        in_specs=(
            P(None, "gx", "gy"),
            P(None, "gx", "gy"),
            P("gx", "gy"),
            P(None, ("gx", "gy"), None),
            P(None, ("gx", "gy"), None),
            P(("gx", "gy"), None),
        ),
        out_specs=(P(None, "gx", "gy"), P(None, ("gx", "gy"), None), P()),
        check_vma=False,
    )
```

profile of v0, /device:TPU:0, one launch (start us, length us, event | category | flops | bytes accessed | tf_op | source)
XLA Modules:
  0.0 58.4 jit_solution(14779750119073099166)
XLA Ops:
  0.6 53.0 %shard_map.85 = (f32[3,256,512]{2,1,0:T(8,128)}, f32[3,16,2048]{2,1,0:T(8,128)}, f32[8,128]{1,0:T(8,128)}) custom-call(f32[3,256,512]{2,1,0:T(8,128)} %fine_start.1, f32[3,256,512]{2,1,0:T(8,128)} %fine_known.1, f32[256,512]{1,0:T(8,128)} %fine_mu.1, f32[3,16,2048]{2,1,0:T(8,128)} %coarse_start.1, f32[3,16,2048]{2,1,0:T(8,128)} %coarse_known.1, ...), custom_call_target="tpu_custom_call" | custom-call | tf_op jit(solution)/shard_map/pallas_call | solution.py:675
  53.6 1.3 %slice_reduce_fusion = f32[3]{0:T(128)} fusion(f32[8,128]{1,0:T(8,128)} %get-tuple-element.8), kind=kLoop, calls=%fused_computation | loop fusion | bytes 24 | tf_op jit(solution)/shard_map/slice | solution.py:734
  54.9 0.0 copy-start
  54.9 2.7 %copy.11 = f32[3,256,512]{2,1,0:T(8,128)} copy(f32[3,256,512]{2,1,0:T(8,128)} %get-tuple-element.12) | data formatting | bytes 3145728
  57.7 0.0 copy-done
  57.7 0.7 %copy.12 = f32[3,16,2048]{2,1,0:T(8,128)} copy(f32[3,16,2048]{2,1,0:T(8,128)S(1)} %copy-done) | data formatting | bytes 786432
Async XLA Ops:
  54.9 2.7 %copy-start = (f32[3,16,2048]{2,1,0:T(8,128)S(1)}, f32[3,16,2048]{2,1,0:T(8,128)}, u32[]{:S(2)}) copy-start(f32[3,16,2048]{2,1,0:T(8,128)} %get-tuple-element.13) | copy-start | bytes 1179652
where the time goes:
time: 58.6 us; the launch traced here: 58.4 us
  Pallas kernels  53 us (90%)
  local copies, waits for them, and re-layouts  4.77 us (8%)
  between operations  0.64 us (1%)
    pallas_call x1, Pallas kernels, on_device(): pl.pallas_call(functools.partial(kernel, n_gx, n_gy, cells_total), out_sh...  53 us
    unnamed x4, local copies, waits for them, and re-layouts  3.47 us
    slice x1, local copies, waits for them, and re-layouts, on_device(): return (fine_ghost, coarse_ghost, norms[:ITERS, 0])  1.31 us

commit v1 on v0

v1 whole, which is shorter than its diff:
```python
import functools

import jax
import jax.numpy as jnp
from jax import lax
from jax.experimental import pallas as pl
from jax.experimental.pallas import tpu as pltpu
from jax.sharding import PartitionSpec as P

ITERS = 3
LANES = 128
SUB = 8
HALF = LANES // 2
AHEAD_CENTRAL = 2
AHEAD_OUTER = 2
VMEM_BYTES = 67043328
MESH = pl.DeviceIdType.MESH
DIRECTIONS = ((-1, 0), (1, 0), (0, -1), (0, 1), (-1, -1), (1, 1), (-1, 1), (1, -1))


def lane_index():
    return lax.broadcasted_iota(jnp.int32, (SUB, LANES), 1)


def roll_lanes(cells, shift):
    shift = shift % LANES
    return cells if shift == 0 else pltpu.roll(cells, shift, 1)


def from_left(halves, halo):
    first = lane_index() == 0
    rolled = [roll_lanes(cells, 1) for cells in halves]
    return [jnp.where(first, before, own) for before, own in zip([halo] + rolled[:-1], rolled)]


def from_right(halves, halo):
    last = lane_index() == LANES - 1
    rolled = [roll_lanes(cells, LANES - 1) for cells in halves]
    return [jnp.where(last, after, own) for own, after in zip(rolled, rolled[1:] + [halo])]


def spread_rows(*rows):
    share = LANES // len(rows)
    return jnp.concatenate(
        [jnp.broadcast_to(row, (share, row.shape[1])) for row in rows], axis=0
    ).T


def kernel(
    n_gx,
    n_gy,
    cells_total,
    fine_start,
    fine_known,
    fine_mu,
    coarse_start,
    coarse_known,
    coarse_mu,
    fine_out,
    coarse_out,
    norms_out,
    raw_start,
    raw_known,
    raw_mu,
    fine_a,
    fine_b,
    known,
    diag,
    inverse,
    patch_start,
    patch_known,
    patch_mu,
    patch_inverse,
    coarse_a,
    coarse_b,
    patch_out,
    fine_row_send,
    fine_row_recv,
    fine_col_send,
    fine_col_recv,
    row_send,
    row_recv,
    col_send,
    col_recv,
    corner_recv,
    fine_halo,
    coarse_halo,
    norm_all,
    tally,
    load_sem,
    move_send,
    move_recv,
    fine_send,
    fine_recv,
    halo_send,
    halo_recv,
    back_send,
    back_recv,
    norm_send,
    norm_recv,
):
    gx = lax.axis_index("gx")
    gy = lax.axis_index("gy")
    me = gx * n_gy + gy
    count = n_gx * n_gy
    central = jnp.logical_and(4 * gy >= n_gy, 4 * gy < 3 * n_gy)
    fine, coarse = (fine_a, fine_b), (coarse_a, coarse_b)
    comps, rows, width = patch_start.shape
    halves = width // LANES
    tiles = 2 * halves
    blocks = rows // SUB
    own_rows = coarse_start.shape[1]
    lane = lane_index()
    barrier = pltpu.get_barrier_semaphore()

    def each_device(action):
        def along_gx(dx, carry):
            def along_gy(dy, inner_carry):
                action({"gx": lax.rem(gx + dx, n_gx), "gy": lax.rem(gy + dy, n_gy)})
                return inner_carry

            return lax.fori_loop(jnp.where(dx == 0, 1, 0), n_gy, along_gy, carry)

        lax.fori_loop(0, n_gx, along_gx, 0)

    each_device(
        lambda peer: pl.semaphore_signal(barrier, inc=1, device_id=peer, device_id_type=MESH)
    )

    loads = []
    for which, (source, target) in enumerate(
        ((fine_start, raw_start), (fine_mu, raw_mu), (fine_known, raw_known))
    ):
        for tile in range(tiles):
            at = pl.ds(tile * LANES, LANES)
            view = source.at[:, at] if len(source.shape) == 2 else source.at[:, :, at]
            loads.append(
                pltpu.make_async_copy(view, target.at[tile], load_sem.at[which])
            )
    for copy in loads:
        copy.start()

    def wait_bytes(ref, sem):
        pltpu.make_async_copy(ref, ref, sem).wait()

    def wait_sent(ref, sem):
        pltpu.make_async_remote_copy(
            ref, ref, sem, sem, device_id={"gy": gy}, device_id_type=MESH
        ).wait_send()

    def clear(edge, refs, corners):
        @pl.when(edge)
        def _():
            for ref, way in refs:
                for sweep in range(ITERS):
                    for comp in range(comps):
                        at = ref.at[sweep, comp, way]
                        at[...] = jnp.zeros_like(at)
            for corner in corners:
                for sweep in range(ITERS):
                    for comp in range(comps):
                        at = corner_recv.at[sweep, comp, corner]
                        at[...] = jnp.zeros_like(at)

    clear(gx == 0, ((row_recv, 0), (fine_row_recv, 0)), (0, 2))
    clear(gx == n_gx - 1, ((row_recv, 1), (fine_row_recv, 1)), (1, 3))
    clear(gy == 0, ((col_recv, 0), (fine_col_recv, 0)), (0, 3))
    clear(gy == n_gy - 1, ((col_recv, 1), (fine_col_recv, 1)), (1, 2))

    pl.semaphore_wait(barrier, count - 1)

    def inside(direction):
        dx, dy = DIRECTIONS[direction]
        checks = []
        if dx:
            checks.append(gx > 0 if dx < 0 else gx < n_gx - 1)
        if dy:
            checks.append(gy > 0 if dy < 0 else gy < n_gy - 1)
        return functools.reduce(jnp.logical_and, checks)

    START, MU, KNOWN = 0, comps, comps + 1

    def plane(item, owner, place):
        columns = pl.ds(pl.multiple_of(owner * width, LANES), width)
        lines = pl.ds(pl.multiple_of(place * own_rows, SUB), own_rows)
        if item == MU:
            return coarse_mu.at[:, columns], patch_mu.at[lines, :]
        comp = item - START if item < MU else item - KNOWN
        source, target = (
            (coarse_start, patch_start) if item < MU else (coarse_known, patch_known)
        )
        return source.at[comp, :, columns], target.at[comp, lines, :]

    def each_step(action):
        def body(step, carry):
            action(lax.rem(gy + step, n_gy))
            return carry

        lax.fori_loop(1, n_gy, body, 0)

    def send_moves(item):
        kind = 0 if item < MU else 1 if item == MU else 2

        def send(peer):
            pltpu.make_async_remote_copy(
                *plane(item, peer, gy),
                move_send.at[kind],
                move_recv.at[item],
                device_id={"gy": peer},
                device_id_type=MESH,
            ).start()

        each_step(send)
        pltpu.make_async_copy(*plane(item, gy, gy), move_recv.at[item]).start()

    def wait_moves(item):
        if item == MU:
            target = patch_mu
        elif item < MU:
            target = patch_start.at[item - START]
        else:
            target = patch_known.at[item - KNOWN]
        wait_bytes(target, move_recv.at[item])

    items = 2 * comps + 1

    def open_moves():
        for item in range(1, AHEAD_CENTRAL):
            send_moves(item)

        @pl.when(jnp.logical_not(central))
        def _():
            for item in range(AHEAD_CENTRAL, AHEAD_OUTER):
                send_moves(item)

    def next_moves(item):
        if item + AHEAD_CENTRAL < items:

            @pl.when(central)
            def _():
                send_moves(item + AHEAD_CENTRAL)

        if item + AHEAD_OUTER < items:

            @pl.when(jnp.logical_not(central))
            def _():
                send_moves(item + AHEAD_OUTER)

    half_lane = lane < HALF
    evens_first = jnp.where(half_lane, 2 * lane, 2 * lane - LANES + 1)
    odds_first = jnp.where(half_lane, 2 * lane + 1, 2 * lane - LANES)

    def split_columns(a, b):
        a = jnp.take_along_axis(a, evens_first, axis=1)
        b = jnp.take_along_axis(b, odds_first, axis=1)
        return (
            jnp.where(half_lane, a, b),
            pltpu.roll(jnp.where(half_lane, b, a), HALF, 1),
        )

    def rows_of(block, shift=0):
        if shift == 0:
            return pl.ds(pl.multiple_of(block * SUB + SUB, SUB), SUB)
        return pl.ds(block * SUB + SUB + shift, SUB)

    def plain(block):
        return pl.ds(pl.multiple_of(block * SUB, SUB), SUB)

    inner = pl.ds(SUB, rows)

    def split_field(raw, comp, put):
        def body(block, carry):
            out = []
            for parity in range(2):
                for half in range(halves):
                    at = pl.ds(block * 2 * SUB + parity, SUB, stride=2)
                    both = split_columns(raw[2 * half, comp, at, :], raw[2 * half + 1, comp, at, :])
                    out.append((parity, half, both))
            for parity, half, both in out:
                put(parity, 0, half, block, both[0])
                put(parity, 1, half, block, both[1])
            return carry

        lax.fori_loop(0, blocks, body, 0, unroll=4)

    def split_start(comp):
        def put(parity, side, half, block, cells):
            fine[0][comp, parity, side, half, rows_of(block), :] = cells

        split_field(raw_start, comp, put)

    def split_known(comp):
        def put(parity, side, half, block, cells):
            known[comp, parity, side, half, plain(block), :] = cells

        split_field(raw_known, comp, put)

    def split_mu(block, carry):
        out = []
        for parity in range(2):
            for half in range(halves):
                at = pl.ds(block * 2 * SUB + parity, SUB, stride=2)
                both = split_columns(raw_mu[2 * half, at, :], raw_mu[2 * half + 1, at, :])
                for side in range(2):
                    total = both[side] + 1.0
                    out.append((parity, side, half, total, 1.0 / total))
        for parity, side, half, total, reciprocal in out:
            diag[parity, side, half, plain(block), :] = total
            inverse[parity, side, half, plain(block), :] = reciprocal
        return carry

    def place_mu():
        def body(block, carry):
            total = patch_mu[plain(block), :] + 1.0
            patch_mu[plain(block), :] = total
            patch_inverse[plain(block), :] = 1.0 / total
            return carry

        lax.fori_loop(0, blocks, body, 0, unroll=4)

    def place_start(comp):
        for half in range(halves):
            coarse[0][comp, half, inner, :] = patch_start[
                comp, :, half * LANES : (half + 1) * LANES
            ]

    def message(rows_out, rows_in, cols_out, cols_in, sends, recvs, sweep, comp, direction):
        dx, dy = DIRECTIONS[direction]
        way = direction % 2
        if direction < 2:
            source, target = rows_out.at[sweep, comp, way], rows_in.at[sweep, comp, 1 - way]
        elif direction < 4:
            source, target = cols_out.at[sweep, comp, way], cols_in.at[sweep, comp, 1 - way]
        else:
            source = rows_out.at[sweep, comp, 0 if dx < 0 else 1]
            target = corner_recv.at[sweep, comp, (direction ^ 1) - 4]
        return pltpu.make_async_remote_copy(
            source,
            target,
            sends.at[direction],
            recvs.at[sweep, comp],
            device_id={"gx": gx + dx, "gy": gy + dy},
            device_id_type=MESH,
        )

    fine_message = functools.partial(
        message, fine_row_send, fine_row_recv, fine_col_send, fine_col_recv, fine_send, fine_recv
    )
    coarse_message = functools.partial(
        message, row_send, row_recv, col_send, col_recv, halo_send, halo_recv
    )

    def start_all(of, sweep, comp, directions):
        for direction in directions:

            @pl.when(inside(direction))
            def _():
                of(sweep, comp, direction).start()

    def wait_all(sem, row_units, col_units, corner_units):
        edge_x = jnp.logical_or(gx == 0, gx == n_gx - 1)
        edge_y = jnp.logical_or(gy == 0, gy == n_gy - 1)
        for sides_x, at_x in ((1, edge_x), (2, jnp.logical_not(edge_x))):
            for sides_y, at_y in ((1, edge_y), (2, jnp.logical_not(edge_y))):

                @pl.when(jnp.logical_and(at_x, at_y))
                def _():
                    units = (
                        row_units * sides_x + col_units * sides_y + corner_units * sides_x * sides_y
                    )
                    wait_bytes(tally.at[pl.ds(0, units)], sem)

    all_lanes = lax.broadcasted_iota(jnp.int32, (rows, LANES), 1)
    low = all_lanes < HALF
    middle = jnp.logical_and(all_lanes >= HALF // 2, all_lanes < HALF + HALF // 2)

    def send_fine_cols(sweep, comp):
        buf = sweep % 2
        parts = []
        for parity in range(2):
            if sweep == 0:
                at = pl.ds(parity, rows, stride=2)
                left, right = raw_start[0, comp, at, :], raw_start[tiles - 1, comp, at, :]
            else:
                left = fine[buf][comp, parity, 0, 0, inner, :]
                right = fine[buf][comp, parity, 1, halves - 1, inner, :]
            parts.append(jnp.where(low, left, right))
        turned = jnp.where(middle, pltpu.roll(parts[1], HALF, 1), parts[0]).T
        for way, lines in enumerate(((0, HALF), (LANES - 1, HALF - 1))):
            for parity, line in enumerate(lines):
                fine_col_send[sweep, comp, way, parity : parity + 1, :] = turned[line : line + 1]
        start_all(fine_message, sweep, comp, (2, 3))

    def send_fine_rows(sweep, comp):
        buf = sweep % 2
        for way, line in enumerate((SUB, SUB + rows - 1)):
            for half in range(halves):
                for side in range(2):
                    at = 2 * half + side
                    fine_row_send[sweep, comp, way, at : at + 1, :] = fine[buf][
                        comp, way, side, half, line : line + 1, :
                    ]
        start_all(fine_message, sweep, comp, (0, 1))

    def send_fine(sweep, comp):
        send_fine_cols(sweep, comp)
        send_fine_rows(sweep, comp)

    def take_fine(sweep, comp):
        buf = sweep % 2
        wait_all(fine_recv.at[sweep, comp], tiles, 2 * rows // LANES, 0)
        for half in range(halves):
            for side in range(2):
                at = 2 * half + side
                fine[buf][comp, 1, side, half, SUB - 1 : SUB, :] = fine_row_recv[
                    sweep, comp, 0, at : at + 1, :
                ]
                fine[buf][comp, 0, side, half, SUB + rows : SUB + rows + 1, :] = fine_row_recv[
                    sweep, comp, 1, at : at + 1, :
                ]
        got = [
            [fine_col_recv[sweep, comp, way, p : p + 1, :] for p in range(2)] for way in range(2)
        ]
        fine_halo[comp] = spread_rows(got[0][0], got[1][1], got[0][1], got[1][0])

    def send_coarse(sweep, comp):
        buf = sweep % 2
        for way, line in enumerate((SUB, SUB + rows - 1)):
            for half in range(halves):
                row_send[sweep, comp, way, half : half + 1, :] = coarse[buf][
                    comp, half, line : line + 1, :
                ]
        start_all(coarse_message, sweep, comp, (0, 1, 4, 5, 6, 7))
        turned = jnp.where(
            low, coarse[buf][comp, 0, inner, :], coarse[buf][comp, halves - 1, inner, :]
        ).T
        col_send[sweep, comp, 0] = turned[0:1]
        col_send[sweep, comp, 1] = turned[LANES - 1 : LANES]
        start_all(coarse_message, sweep, comp, (2, 3))

    first_row = lax.broadcasted_iota(jnp.int32, (1, LANES), 1) < HALF

    def take_coarse(sweep, comp):
        buf = sweep % 2
        wait_all(halo_recv.at[sweep, comp], halves, rows // LANES, halves)
        for way, line in enumerate((SUB - 1, SUB + rows)):
            for half in range(halves):
                coarse[buf][comp, half, line : line + 1, :] = row_recv[
                    sweep, comp, way, half : half + 1, :
                ]
        coarse_halo[comp, inner, :] = spread_rows(
            col_recv[sweep, comp, 0], col_recv[sweep, comp, 1]
        )
        for (before, after), line in zip(((0, 2), (3, 1)), (SUB - 1, SUB + rows)):
            left = corner_recv[sweep, comp, before, halves - 1 : halves, :]
            right = corner_recv[sweep, comp, after, 0:1, :]
            coarse_halo[comp, line : line + 1, :] = jnp.where(
                first_row, pltpu.roll(left, 1, 1), pltpu.roll(right, LANES - 1, 1)
            )

    zero = jnp.zeros((SUB, LANES), jnp.float32)

    def coarse_pass(sweep, comp):
        buf = sweep % 2
        last = sweep == ITERS - 1

        def body(block, totals):
            totals = list(totals)
            lines = plain(block)
            out = []
            halo = coarse_halo[comp, rows_of(block), :]
            own = [coarse[buf][comp, half, rows_of(block), :] for half in range(halves)]
            lefts, rights = from_left(own, halo), from_right(own, halo)
            for half in range(halves):
                columns = slice(half * LANES, (half + 1) * LANES)
                near = (
                    coarse[buf][comp, half, rows_of(block, 1), :]
                    + coarse[buf][comp, half, rows_of(block, -1), :]
                    + rights[half]
                    + lefts[half]
                )
                below = (
                    fine[buf][comp, 0, 0, half, rows_of(block), :]
                    + fine[buf][comp, 1, 0, half, rows_of(block), :]
                    + fine[buf][comp, 0, 1, half, rows_of(block), :]
                    + fine[buf][comp, 1, 1, half, rows_of(block), :]
                )
                res = (
                    patch_known[comp, lines, columns]
                    + 0.25 * near
                    + 0.125 * below
                    - patch_mu[lines, columns] * own[half]
                )
                totals[half % 2] = totals[half % 2] + res * res
                out.append((half, own[half] + res * patch_inverse[lines, columns]))
            for half, new in out:
                if last:
                    patch_out[comp, lines, half * LANES : (half + 1) * LANES] = new
                else:
                    coarse[1 - buf][comp, half, rows_of(block), :] = new
            return tuple(totals)

        return sum(lax.fori_loop(0, blocks, body, (zero,) * 2, unroll=4))

    def fine_pass(sweep, comp):
        buf = sweep % 2

        def body(block, totals):
            totals = list(totals)
            out = []
            mid = [coarse[buf][comp, half, rows_of(block), :] for half in range(halves)]
            mid_halo = coarse_halo[comp, rows_of(block), :]
            fine_edges = fine_halo[comp, plain(block), :]
            for parity in range(2):
                shift = 1 if parity else -1
                far_halo = coarse_halo[comp, rows_of(block, shift), :]
                line = [
                    0.75 * mid[half] + 0.25 * coarse[buf][comp, half, rows_of(block, shift), :]
                    for half in range(halves)
                ]
                line_halo = 0.75 * mid_halo + 0.25 * far_halo
                line_left, line_right = from_left(line, line_halo), from_right(line, line_halo)
                edge = roll_lanes(fine_edges, HALF) if parity else fine_edges
                evens, odds = (
                    [fine[buf][comp, parity, side, half, rows_of(block), :] for half in range(halves)]
                    for side in range(2)
                )
                before, after = from_left(odds, edge), from_right(evens, edge)
                for half in range(halves):
                    for side in range(2):
                        own = odds[half] if side else evens[half]
                        lateral = evens[half] + after[half] if side else odds[half] + before[half]
                        near = (
                            fine[buf][comp, 1 - parity, side, half, rows_of(block), :]
                            + fine[buf][comp, 1 - parity, side, half, rows_of(block, shift), :]
                            + lateral
                        )
                        spread = 0.75 * line[half] + 0.25 * (
                            line_right[half] if side else line_left[half]
                        )
                        res = (
                            known[comp, parity, side, half, plain(block), :]
                            + 0.25 * near
                            + 0.5 * spread
                            - diag[parity, side, half, plain(block), :] * own
                        )
                        at = 2 * parity + side
                        totals[at] = totals[at] + res * res
                        new = own + res * inverse[parity, side, half, plain(block), :]
                        out.append((parity, side, half, new))
            for parity, side, half, new in out:
                fine[1 - buf][comp, parity, side, half, rows_of(block), :] = new
            return tuple(totals)

        return sum(lax.fori_loop(0, blocks, body, (zero,) * 4, unroll=2))

    def back_rows(owner):
        return pl.ds(pl.multiple_of(owner * own_rows, SUB), own_rows)

    def back_columns(place):
        return pl.ds(pl.multiple_of(place * width, LANES), width)

    def send_back(comp):
        def send(peer):
            pltpu.make_async_remote_copy(
                patch_out.at[comp, back_rows(peer), :],
                coarse_out.at[comp, :, back_columns(gy)],
                back_send.at[0],
                back_recv.at[0],
                device_id={"gy": peer},
                device_id_type=MESH,
            ).start()

        each_step(send)
        coarse_out[comp, :, back_columns(gy)] = patch_out[comp, back_rows(gy), :]

    weave_a = jnp.where(lane % 2 == 0, lane // 2, lane // 2 + HALF)
    weave_b = jnp.where(lane % 2 == 0, lane // 2 + HALF, lane // 2)
    final = ITERS % 2

    def weave(comp):
        def body(block, carry):
            out = []
            for parity in range(2):
                for half in range(halves):
                    even = fine[final][comp, parity, 0, half, rows_of(block), :]
                    odd = fine[final][comp, parity, 1, half, rows_of(block), :]
                    odd = pltpu.roll(odd, HALF, 1)
                    at = pl.ds(block * 2 * SUB + parity, SUB, stride=2)
                    a = jnp.take_along_axis(jnp.where(half_lane, even, odd), weave_a, axis=1)
                    b = jnp.take_along_axis(jnp.where(half_lane, odd, even), weave_b, axis=1)
                    out.append((2 * half, at, a))
                    out.append((2 * half + 1, at, b))
            for tile, at, cells in out:
                fine_out[tile, comp, at, :] = cells
            return carry

        lax.fori_loop(0, blocks, body, 0, unroll=4)

    totals = [zero] * ITERS

    def on_coarse(sweep, comp):
        totals[sweep] = totals[sweep] + coarse_pass(sweep, comp)

    def on_fine(sweep, comp):
        totals[sweep] = totals[sweep] + fine_pass(sweep, comp)

    def place(comp):
        wait_moves(START + comp)
        place_start(comp)
        send_coarse(0, comp)

    def first_fine(comp):
        take_fine(0, comp)
        take_coarse(0, comp)
        on_fine(0, comp)
        send_fine(1, comp)

    send_moves(START)
    wait_bytes(raw_start, load_sem.at[0])
    for comp in range(comps):
        send_fine_cols(0, comp)
    open_moves()
    for comp in range(comps):
        split_start(comp)
        send_fine_rows(0, comp)
    wait_bytes(raw_mu, load_sem.at[1])
    lax.fori_loop(0, blocks, split_mu, 0, unroll=2)
    wait_bytes(raw_known, load_sem.at[2])
    place(0)
    next_moves(0)
    split_known(0)
    place(1)
    next_moves(1)
    first_fine(0)
    split_known(1)
    place(2)
    next_moves(2)
    first_fine(1)
    split_known(2)
    first_fine(2)
    wait_moves(MU)
    next_moves(MU)
    place_mu()

    def first_coarse(comp):
        wait_moves(KNOWN + comp)
        on_coarse(0, comp)
        send_coarse(1, comp)
        next_moves(KNOWN + comp)

    def second_coarse(comp):
        take_coarse(1, comp)
        on_coarse(1, comp)
        send_coarse(2, comp)

    def second_fine(comp):
        take_fine(1, comp)
        on_fine(1, comp)
        send_fine(2, comp)

    def last_coarse(comp):
        take_coarse(2, comp)
        on_coarse(2, comp)
        send_back(comp)

    def last_fine(comp):
        take_fine(2, comp)
        on_fine(2, comp)

    one_lane = lax.broadcasted_iota(jnp.int32, (1, LANES), 1)

    def gather_sum(sums, sweep):
        return jnp.where(one_lane == sweep, jnp.sum(totals[sweep]), sums)

    first_coarse(0)
    first_coarse(1)
    second_coarse(0)
    second_fine(0)
    first_coarse(2)
    second_coarse(1)
    last_coarse(0)
    second_fine(1)
    second_coarse(2)
    last_coarse(1)
    second_fine(2)
    last_fine(0)
    last_coarse(2)
    sums = jnp.zeros((1, LANES), jnp.float32)
    for sweep in range(ITERS - 1):
        sums = gather_sum(sums, sweep)
    last_fine(1)
    last_fine(2)
    norm_all[me] = gather_sum(sums, ITERS - 1)
    each_device(
        lambda peer: pltpu.make_async_remote_copy(
            norm_all.at[me],
            norm_all.at[me],
            norm_send.at[0],
            norm_recv.at[0],
            device_id=peer,
            device_id_type=MESH,
        ).start()
    )
    for comp in range(comps):
        weave(comp)

    for direction in range(8):
        way = direction % 2 if direction < 4 else 0 if DIRECTIONS[direction][0] < 0 else 1

        @pl.when(inside(direction))
        def _():
            sent = (col_send if direction in (2, 3) else row_send).at[:, :, way]
            wait_sent(sent, halo_send.at[direction])
            if direction < 4:
                sent = (fine_col_send if direction > 1 else fine_row_send).at[:, :, way]
                wait_sent(sent, fine_send.at[direction])

    others = pl.ds(0, rows - own_rows)
    wait_sent(patch_start.at[:, others, :], move_send.at[0])
    wait_sent(patch_mu.at[others, :], move_send.at[1])
    wait_sent(patch_known.at[:, others, :], move_send.at[2])
    wait_sent(patch_out.at[:, others, :], back_send.at[0])
    rest = norm_all.at[pl.ds(0, count - 1)]
    wait_sent(rest, norm_send.at[0])
    wait_bytes(rest, norm_recv.at[0])
    whole = lax.fori_loop(
        0, count, lambda i, acc: acc + norm_all[i], jnp.zeros((1, LANES), jnp.float32)
    )
    norms_out[...] = jnp.broadcast_to(jnp.sqrt(whole / cells_total), norms_out.shape)
    wait_bytes(coarse_out.at[:, :, pl.ds(0, (n_gy - 1) * width)], back_recv.at[0])


def finish(fine_in, coarse_in, norms_in, fine_out, coarse_out, norms_out, sems):
    tiles = fine_in.shape[0]
    copies = [pltpu.make_async_copy(coarse_in, coarse_out, sems.at[tiles])]
    for tile in range(tiles):
        copies.append(
            pltpu.make_async_copy(
                fine_in.at[tile], fine_out.at[:, :, pl.ds(tile * LANES, LANES)], sems.at[tile]
            )
        )
    for copy in copies:
        copy.start()
    for sweep in range(ITERS):
        norms_out[sweep] = norms_in[0, sweep]
    for copy in copies:
        copy.wait()


def on_device(n_gx, n_gy, fine_start, fine_known, fine_mu, coarse_start, coarse_known, coarse_mu):
    comps, fine_rows, fine_cols = fine_start.shape
    rows, width = fine_rows // 2, fine_cols // 2
    halves = width // LANES
    tiles = 2 * halves
    padded = rows + 2 * SUB
    cells_total = 3.0 * (fine_mu.size + coarse_mu.size) * n_gx * n_gy
    f32 = jnp.float32
    dma = pltpu.SemaphoreType.DMA
    anywhere = pl.BlockSpec(memory_space=pl.ANY)
    in_vmem = pl.BlockSpec(memory_space=pltpu.VMEM)
    out_bytes = 4 * (fine_start.size + coarse_start.size + SUB * LANES)
    results = pl.pallas_call(
        functools.partial(kernel, n_gx, n_gy, cells_total),
        out_shape=(
            pltpu.VMEM((tiles, comps, fine_rows, LANES), f32),
            pltpu.VMEM(coarse_start.shape, f32),
            pltpu.VMEM((SUB, LANES), f32),
        ),
        in_specs=[pl.BlockSpec(memory_space=pltpu.HBM)] * 6,
        out_specs=(in_vmem,) * 3,
        scratch_shapes=[
            pltpu.VMEM((tiles, comps, fine_rows, LANES), f32),
            pltpu.VMEM((tiles, comps, fine_rows, LANES), f32),
            pltpu.VMEM((tiles, fine_rows, LANES), f32),
            pltpu.VMEM((comps, 2, 2, halves, padded, LANES), f32),
            pltpu.VMEM((comps, 2, 2, halves, padded, LANES), f32),
            pltpu.VMEM((comps, 2, 2, halves, rows, LANES), f32),
            pltpu.VMEM((2, 2, halves, rows, LANES), f32),
            pltpu.VMEM((2, 2, halves, rows, LANES), f32),
            pltpu.VMEM((comps, rows, width), f32),
            pltpu.VMEM((comps, rows, width), f32),
            pltpu.VMEM((rows, width), f32),
            pltpu.VMEM((rows, width), f32),
            pltpu.VMEM((comps, halves, padded, LANES), f32),
            pltpu.VMEM((comps, halves, padded, LANES), f32),
            pltpu.VMEM((comps, rows, width), f32),
            pltpu.VMEM((ITERS, comps, 2, tiles, LANES), f32),
            pltpu.VMEM((ITERS, comps, 2, tiles, LANES), f32),
            pltpu.VMEM((ITERS, comps, 2, 2, rows), f32),
            pltpu.VMEM((ITERS, comps, 2, 2, rows), f32),
            pltpu.VMEM((ITERS, comps, 2, halves, LANES), f32),
            pltpu.VMEM((ITERS, comps, 2, halves, LANES), f32),
            pltpu.VMEM((ITERS, comps, 2, 1, rows), f32),
            pltpu.VMEM((ITERS, comps, 2, 1, rows), f32),
            pltpu.VMEM((ITERS, comps, 4, halves, LANES), f32),
            pltpu.VMEM((comps, rows, LANES), f32),
            pltpu.VMEM((comps, padded, LANES), f32),
            pltpu.VMEM((n_gx * n_gy, 1, LANES), f32),
            pltpu.VMEM((6 * halves + 4 * rows // LANES, 1, LANES), f32),
            dma((3,)),
            dma((3,)),
            dma((2 * comps + 1,)),
            dma((4,)),
            dma((ITERS, comps)),
            dma((8,)),
            dma((ITERS, comps)),
            dma((1,)),
            dma((1,)),
            dma((1,)),
            dma((1,)),
        ],
        compiler_params=pltpu.CompilerParams(
            collective_id=0,
            has_side_effects=True,
            vmem_limit_bytes=VMEM_BYTES - out_bytes - 2 * SUB * LANES * 4,
        ),
    )(fine_start, fine_known, fine_mu, coarse_start, coarse_known, coarse_mu)
    return pl.pallas_call(
        finish,
        out_shape=(
            jax.ShapeDtypeStruct(fine_start.shape, f32),
            jax.ShapeDtypeStruct(coarse_start.shape, f32),
            jax.ShapeDtypeStruct((ITERS,), f32),
        ),
        in_specs=[in_vmem] * 3,
        out_specs=(anywhere, anywhere, pl.BlockSpec(memory_space=pltpu.SMEM)),
        scratch_shapes=[dma((tiles + 1,))],
        compiler_params=pltpu.CompilerParams(vmem_limit_bytes=2**20),
    )(*(pltpu.with_memory_space_constraint(result, pltpu.VMEM) for result in results))


def solution(mesh):
    n_gx, n_gy = mesh.shape["gx"], mesh.shape["gy"]
    return jax.shard_map(
        functools.partial(on_device, n_gx, n_gy),
        mesh=mesh,
        in_specs=(
            P(None, "gx", "gy"),
            P(None, "gx", "gy"),
            P("gx", "gy"),
            P(None, ("gx", "gy"), None),
            P(None, ("gx", "gy"), None),
            P(("gx", "gy"), None),
        ),
        out_specs=(P(None, "gx", "gy"), P(None, ("gx", "gy"), None), P()),
        check_vma=False,
    )
```

time: 58.6 us -> 51 us (0.87)
  local copies, waits for them, and re-layouts: 4.77 us -> 0 us
  Pallas kernels: 53 us -> 50.2 us
    pallas_call x1, Pallas kernels: 53 us -> 48.4 us  [on_device(): pl.pallas_call(functools.partial(kernel, n_gx, n_gy, cells_total), out_sh...]
    unnamed x4 -> x0, local copies, waits for them, and re-layouts: 3.47 us -> none
    pallas_call x0 -> x1, Pallas kernels: none -> 1.82 us  [on_device(): pl.pallas_call(finish, out_shape=(jax.ShapeDtypeStruct(fine_start.shape,...]
    slice x1 -> x0, local copies, waits for them, and re-layouts: 1.31 us -> none  [on_device(): return (fine_ghost, coarse_ghost, norms[:ITERS, 0])]
where the time goes in v1:
time: 51 us; the launch traced here: 50.9 us
  Pallas kernels  50.2 us (98%)
  between operations  0.64 us (1%)
    pallas_call x1, Pallas kernels, on_device(): pl.pallas_call(functools.partial(kernel, n_gx, n_gy, cells_total), out_sh...  48.4 us
    pallas_call x1, Pallas kernels, on_device(): pl.pallas_call(finish, out_shape=(jax.ShapeDtypeStruct(fine_start.shape,...  1.82 us

profile of v1, /device:TPU:0, one launch (start us, length us, event | category | flops | bytes accessed | tf_op | source)
XLA Modules:
  0.0 50.9 jit_solution(7190047625262154127)
XLA Ops:
  0.6 48.4 %shard_map.85 = (f32[4,3,256,128]{3,2,1,0:T(8,128)S(1)}, f32[3,16,2048]{2,1,0:T(8,128)S(1)}, f32[8,128]{1,0:T(8,128)S(1)}) custom-call(f32[3,256,512]{2,1,0:T(8,128)} %fine_start.1, f32[3,256,512]{2,1,0:T(8,128)} %fine_known.1, f32[256,512]{1,0:T(8,128)} %fine_mu.1, f32[3,16,2048]{2,1,0:T(8,128)} %coarse_start.1, f32[3,16,2048]{2,1,0:T(8,128)} %coarse_known.1, ...), custom_call_target="tpu_custom_call" | custom-call | tf_op jit(solution)/shard_map/pallas_call | solution.py:763
  49.1 1.8 %shard_map.86 = (f32[3,256,512]{2,1,0:T(8,128)}, f32[3,16,2048]{2,1,0:T(8,128)}, f32[3]{0:T(128)}) custom-call(f32[4,3,256,128]{3,2,1,0:T(8,128)S(1)} %get-tuple-element.6.fine_in, f32[3,16,2048]{2,1,0:T(8,128)S(1)} %get-tuple-element.7.coarse_in, f32[8,128]{1,0:T(8,128)S(1)} %get-tuple-element.8.norms_in), custom_call_target="tpu_custom_call" | custom-call | tf_op jit(solution)/shard_map/pallas_call | solution.py:819

commit v2 on v1

--- a/solution.py
+++ b/solution.py
@@ -11,11 +11,15 @@
 LANES = 128
 SUB = 8
 HALF = LANES // 2
-AHEAD_CENTRAL = 2
-AHEAD_OUTER = 2
 VMEM_BYTES = 67043328
 MESH = pl.DeviceIdType.MESH
-DIRECTIONS = ((-1, 0), (1, 0), (0, -1), (0, 1), (-1, -1), (1, 1), (-1, 1), (1, -1))
+DIRECTIONS = ((-1, 0), (1, 0), (0, -1), (0, 1))
+QUARTER = LANES // 4
+REACH = 4
+FINE_UNROLL = 8
+COARSE_UNROLL = 16
+SPLIT_UNROLL = 8
+MU_UNROLL = 8
 
 
 def lane_index():
@@ -27,23 +31,28 @@
     return cells if shift == 0 else pltpu.roll(cells, shift, 1)
 
 
-def from_left(halves, halo):
+def beside_left(halves, halo):
     first = lane_index() == 0
     rolled = [roll_lanes(cells, 1) for cells in halves]
     return [jnp.where(first, before, own) for before, own in zip([halo] + rolled[:-1], rolled)]
 
 
-def from_right(halves, halo):
+def beside_right(halves, halo):
     last = lane_index() == LANES - 1
     rolled = [roll_lanes(cells, LANES - 1) for cells in halves]
     return [jnp.where(last, after, own) for own, after in zip(rolled, rolled[1:] + [halo])]
 
 
-def spread_rows(*rows):
-    share = LANES // len(rows)
-    return jnp.concatenate(
-        [jnp.broadcast_to(row, (share, row.shape[1])) for row in rows], axis=0
-    ).T
+def from_left(ring):
+    first = lane_index() == 0
+    rolled = [roll_lanes(cells, 1) for cells in ring]
+    return [jnp.where(first, rolled[at - 1], rolled[at]) for at in range(len(ring))]
+
+
+def from_right(ring):
+    last = lane_index() == LANES - 1
+    rolled = [roll_lanes(cells, LANES - 1) for cells in ring]
+    return [jnp.where(last, rolled[at + 1 - len(ring)], rolled[at]) for at in range(len(ring))]
 
 
 def kernel(
@@ -80,11 +89,13 @@
     fine_col_recv,
     row_send,
     row_recv,
-    col_send,
-    col_recv,
-    corner_recv,
     fine_halo,
-    coarse_halo,
+    own_planes,
+    strip_send,
+    strip_recv,
+    strip_known,
+    strip_mu,
+    strip_inverse,
     norm_all,
     tally,
     load_sem,
@@ -98,12 +109,13 @@
     back_recv,
     norm_send,
     norm_recv,
+    edge_send,
+    edge_recv,
 ):
     gx = lax.axis_index("gx")
     gy = lax.axis_index("gy")
     me = gx * n_gy + gy
     count = n_gx * n_gy
-    central = jnp.logical_and(4 * gy >= n_gy, 4 * gy < 3 * n_gy)
     fine, coarse = (fine_a, fine_b), (coarse_a, coarse_b)
     comps, rows, width = patch_start.shape
     halves = width // LANES
@@ -148,24 +160,26 @@
             ref, ref, sem, sem, device_id={"gy": gy}, device_id_type=MESH
         ).wait_send()
 
-    def clear(edge, refs, corners):
+    pltpu.make_async_copy(coarse_start, own_planes.at[pl.ds(0, comps)], load_sem.at[3]).start()
+    pltpu.make_async_copy(coarse_mu, own_planes.at[comps], load_sem.at[3]).start()
+    pltpu.make_async_copy(
+        coarse_known, own_planes.at[pl.ds(comps + 1, comps)], load_sem.at[3]
+    ).start()
+
+    def clear(edge, ref, way):
         @pl.when(edge)
         def _():
-            for ref, way in refs:
-                for sweep in range(ITERS):
-                    for comp in range(comps):
-                        at = ref.at[sweep, comp, way]
-                        at[...] = jnp.zeros_like(at)
-            for corner in corners:
-                for sweep in range(ITERS):
-                    for comp in range(comps):
-                        at = corner_recv.at[sweep, comp, corner]
-                        at[...] = jnp.zeros_like(at)
-
-    clear(gx == 0, ((row_recv, 0), (fine_row_recv, 0)), (0, 2))
-    clear(gx == n_gx - 1, ((row_recv, 1), (fine_row_recv, 1)), (1, 3))
-    clear(gy == 0, ((col_recv, 0), (fine_col_recv, 0)), (0, 3))
-    clear(gy == n_gy - 1, ((col_recv, 1), (fine_col_recv, 1)), (1, 2))
+            for sweep in range(ITERS):
+                for comp in range(comps):
+                    at = ref.at[sweep, comp, way]
+                    at[...] = jnp.zeros_like(at)
+
+    for ref in (row_recv, fine_row_recv):
+        clear(gx == 0, ref, 0)
+        clear(gx == n_gx - 1, ref, 1)
+    clear(gy == 0, fine_col_recv, 0)
+    clear(gy == n_gy - 1, fine_col_recv, 1)
+    row_send[...] = jnp.zeros_like(row_send)
 
     pl.semaphore_wait(barrier, count - 1)
 
@@ -223,30 +237,64 @@
         wait_bytes(target, move_recv.at[item])
 
     items = 2 * comps + 1
-
-    def open_moves():
-        for item in range(1, AHEAD_CENTRAL):
-            send_moves(item)
-
-        @pl.when(jnp.logical_not(central))
-        def _():
-            for item in range(AHEAD_CENTRAL, AHEAD_OUTER):
-                send_moves(item)
-
-    def next_moves(item):
-        if item + AHEAD_CENTRAL < items:
-
-            @pl.when(central)
-            def _():
-                send_moves(item + AHEAD_CENTRAL)
-
-        if item + AHEAD_OUTER < items:
-
-            @pl.when(jnp.logical_not(central))
-            def _():
-                send_moves(item + AHEAD_OUTER)
-
     half_lane = lane < HALF
+    valid = jnp.where(half_lane, jnp.where(gy < n_gy - 1, 1, 0), jnp.where(gy > 0, 1, 0)) == 1
+    own_tiles = own_rows // SUB
+    share = LANES // own_tiles
+
+    def strip_at(tile, item):
+        return tile * share + 2 * REACH * item
+
+    def send_strips():
+        wait_bytes(own_planes, load_sem.at[3])
+        for owner in range(n_gy):
+            cells = jnp.zeros((SUB, LANES), jnp.float32)
+            for tile in range(own_tiles):
+                lines = slice(tile * SUB, (tile + 1) * SUB)
+                for item in range(items):
+                    sides = []
+                    for at in (halves * (owner + 1), halves * owner - 1):
+                        at = at if 0 <= at < n_gy * halves else 0
+                        sides.append(own_planes[item, lines, at * LANES : (at + 1) * LANES])
+                    both = jnp.where(half_lane, *sides)
+                    start = strip_at(tile, item)
+                    here = jnp.logical_and(lane >= start, lane < start + 2 * REACH)
+                    cells = jnp.where(here, roll_lanes(both, start + REACH), cells)
+            strip_send[owner] = cells
+
+        def send(peer):
+            pltpu.make_async_remote_copy(
+                strip_send.at[peer],
+                strip_recv.at[gy],
+                edge_send.at[0],
+                edge_recv.at[0],
+                device_id={"gy": peer},
+                device_id_type=MESH,
+            ).start()
+
+        each_step(send)
+
+    def take_strips():
+        strip_recv[gy] = strip_send[gy]
+        wait_bytes(strip_recv.at[pl.ds(0, n_gy - 1)], edge_recv.at[0])
+
+        def body(owner, carry):
+            cells = strip_recv[owner]
+            for tile in range(own_tiles):
+                block = owner * own_tiles + tile
+                for item in range(items):
+                    strip = roll_lanes(cells, -strip_at(tile, item) - REACH)
+                    if item < MU:
+                        coarse[0][item, halves, rows_of(block), :] = jnp.where(valid, strip, 0.0)
+                    elif item == MU:
+                        strip_mu[plain(block), :] = strip + 1.0
+                        strip_inverse[plain(block), :] = 1.0 / (strip + 1.0)
+                    else:
+                        strip_known[item - KNOWN, plain(block), :] = strip
+            return carry
+
+        lax.fori_loop(0, n_gy, body, 0, unroll=2)
+
     evens_first = jnp.where(half_lane, 2 * lane, 2 * lane - LANES + 1)
     odds_first = jnp.where(half_lane, 2 * lane + 1, 2 * lane - LANES)
 
@@ -281,7 +329,7 @@
                 put(parity, 1, half, block, both[1])
             return carry
 
-        lax.fori_loop(0, blocks, body, 0, unroll=4)
+        lax.fori_loop(0, blocks, body, 0, unroll=SPLIT_UNROLL)
 
     def split_start(comp):
         def put(parity, side, half, block, cells):
@@ -324,72 +372,69 @@
                 comp, :, half * LANES : (half + 1) * LANES
             ]
 
-    def message(rows_out, rows_in, cols_out, cols_in, sends, recvs, sweep, comp, direction):
+    def message(direction, source, target, send, recv):
         dx, dy = DIRECTIONS[direction]
-        way = direction % 2
-        if direction < 2:
-            source, target = rows_out.at[sweep, comp, way], rows_in.at[sweep, comp, 1 - way]
-        elif direction < 4:
-            source, target = cols_out.at[sweep, comp, way], cols_in.at[sweep, comp, 1 - way]
-        else:
-            source = rows_out.at[sweep, comp, 0 if dx < 0 else 1]
-            target = corner_recv.at[sweep, comp, (direction ^ 1) - 4]
-        return pltpu.make_async_remote_copy(
-            source,
-            target,
-            sends.at[direction],
-            recvs.at[sweep, comp],
-            device_id={"gx": gx + dx, "gy": gy + dy},
-            device_id_type=MESH,
-        )
-
-    fine_message = functools.partial(
-        message, fine_row_send, fine_row_recv, fine_col_send, fine_col_recv, fine_send, fine_recv
-    )
-    coarse_message = functools.partial(
-        message, row_send, row_recv, col_send, col_recv, halo_send, halo_recv
-    )
-
-    def start_all(of, sweep, comp, directions):
-        for direction in directions:
-
-            @pl.when(inside(direction))
-            def _():
-                of(sweep, comp, direction).start()
-
-    def wait_all(sem, row_units, col_units, corner_units):
-        edge_x = jnp.logical_or(gx == 0, gx == n_gx - 1)
-        edge_y = jnp.logical_or(gy == 0, gy == n_gy - 1)
-        for sides_x, at_x in ((1, edge_x), (2, jnp.logical_not(edge_x))):
-            for sides_y, at_y in ((1, edge_y), (2, jnp.logical_not(edge_y))):
-
-                @pl.when(jnp.logical_and(at_x, at_y))
-                def _():
-                    units = (
-                        row_units * sides_x + col_units * sides_y + corner_units * sides_x * sides_y
-                    )
-                    wait_bytes(tally.at[pl.ds(0, units)], sem)
+
+        @pl.when(inside(direction))
+        def _():
+            pltpu.make_async_remote_copy(
+                source,
+                target,
+                send.at[direction],
+                recv,
+                device_id={"gx": gx + dx, "gy": gy + dy},
+                device_id_type=MESH,
+            ).start()
+
+    edge_x = jnp.logical_or(gx == 0, gx == n_gx - 1)
+    edge_y = jnp.logical_or(gy == 0, gy == n_gy - 1)
+    sides_x = ((1, edge_x), (2, jnp.logical_not(edge_x)))
+    sides_y = ((1, edge_y), (2, jnp.logical_not(edge_y)))
 
     all_lanes = lax.broadcasted_iota(jnp.int32, (rows, LANES), 1)
     low = all_lanes < HALF
-    middle = jnp.logical_and(all_lanes >= HALF // 2, all_lanes < HALF + HALF // 2)
+    middle = jnp.logical_and(all_lanes >= HALF, all_lanes < HALF + QUARTER)
+    middle = jnp.logical_or(middle, jnp.logical_and(all_lanes >= HALF - SUB, all_lanes < HALF))
+    beside = jnp.logical_and(all_lanes >= QUARTER - REACH, all_lanes < QUARTER + REACH)
 
     def send_fine_cols(sweep, comp):
         buf = sweep % 2
-        parts = []
+        parts, sums = [], []
         for parity in range(2):
             if sweep == 0:
                 at = pl.ds(parity, rows, stride=2)
-                left, right = raw_start[0, comp, at, :], raw_start[tiles - 1, comp, at, :]
+                ends = [raw_start[0, comp, at, :], raw_start[tiles - 1, comp, at, :]]
+                sums.append(ends)
             else:
-                left = fine[buf][comp, parity, 0, 0, inner, :]
-                right = fine[buf][comp, parity, 1, halves - 1, inner, :]
-            parts.append(jnp.where(low, left, right))
-        turned = jnp.where(middle, pltpu.roll(parts[1], HALF, 1), parts[0]).T
-        for way, lines in enumerate(((0, HALF), (LANES - 1, HALF - 1))):
-            for parity, line in enumerate(lines):
-                fine_col_send[sweep, comp, way, parity : parity + 1, :] = turned[line : line + 1]
-        start_all(fine_message, sweep, comp, (2, 3))
+                ends = [
+                    fine[buf][comp, parity, side, half, inner, :]
+                    for side, half in ((0, 0), (1, halves - 1))
+                ]
+                others = [
+                    fine[buf][comp, parity, 1 - side, half, inner, :]
+                    for side, half in ((0, 0), (1, halves - 1))
+                ]
+                sums.append([a + b for a, b in zip(ends, others)])
+            parts.append(jnp.where(low, *ends))
+        total = jnp.where(low, sums[0][0] + sums[1][0], sums[0][1] + sums[1][1])
+        pitch = 1
+        if sweep == 0:
+            total = total + pltpu.roll(total, LANES - 1, 1)
+            pitch = 2
+        mixed = jnp.where(middle, pltpu.roll(parts[1], HALF, 1), parts[0])
+        turned = jnp.where(beside, pltpu.roll(total, QUARTER, 1), mixed).T
+        first = (0, HALF, QUARTER, QUARTER + pitch)
+        last = (LANES - 1, HALF - 1, QUARTER - pitch, QUARTER - 2 * pitch)
+        for way, lines in enumerate((first, last)):
+            for at, line in enumerate(lines):
+                fine_col_send[sweep, comp, way, at : at + 1, :] = turned[line : line + 1]
+            message(
+                2 + way,
+                fine_col_send.at[sweep, comp, way],
+                fine_col_recv.at[sweep, comp, 1 - way],
+                fine_send,
+                fine_recv.at[sweep, comp],
+            )
 
     def send_fine_rows(sweep, comp):
         buf = sweep % 2
@@ -400,15 +445,30 @@
                     fine_row_send[sweep, comp, way, at : at + 1, :] = fine[buf][
                         comp, way, side, half, line : line + 1, :
                     ]
-        start_all(fine_message, sweep, comp, (0, 1))
+            message(
+                way,
+                fine_row_send.at[sweep, comp, way],
+                fine_row_recv.at[sweep, comp, 1 - way],
+                fine_send,
+                fine_recv.at[sweep, comp],
+            )
 
     def send_fine(sweep, comp):
         send_fine_cols(sweep, comp)
         send_fine_rows(sweep, comp)
 
+    line_at = lax.broadcasted_iota(jnp.int32, (SUB, rows), 0)
+
     def take_fine(sweep, comp):
         buf = sweep % 2
-        wait_all(fine_recv.at[sweep, comp], tiles, 2 * rows // LANES, 0)
+        for count_x, at_x in sides_x:
+            for count_y, at_y in sides_y:
+
+                @pl.when(jnp.logical_and(at_x, at_y))
+                def _():
+                    units = tiles * count_x + 4 * rows // LANES * count_y
+                    wait_bytes(tally.at[pl.ds(0, units)], fine_recv.at[sweep, comp])
+
         for half in range(halves):
             for side in range(2):
                 at = 2 * half + side
@@ -418,45 +478,54 @@
                 fine[buf][comp, 0, side, half, SUB + rows : SUB + rows + 1, :] = fine_row_recv[
                     sweep, comp, 1, at : at + 1, :
                 ]
-        got = [
-            [fine_col_recv[sweep, comp, way, p : p + 1, :] for p in range(2)] for way in range(2)
-        ]
-        fine_halo[comp] = spread_rows(got[0][0], got[1][1], got[0][1], got[1][0])
+        left, right = (
+            [
+                jnp.broadcast_to(fine_col_recv[sweep, comp, way, at : at + 1, :], (SUB, rows))
+                for at in range(4)
+            ]
+            for way in range(2)
+        )
+        near_left = jnp.where(line_at == SUB - 1, left[2], left[3])
+        near_right = jnp.where(line_at == 0, right[2], right[3])
+        turned = jnp.concatenate(
+            [left[0]] * 3
+            + [near_left, near_right]
+            + [right[1]] * 3
+            + [left[1]] * 4
+            + [right[0]] * 4,
+            axis=0,
+        )
+        fine_halo[comp] = turned.T
 
     def send_coarse(sweep, comp):
         buf = sweep % 2
         for way, line in enumerate((SUB, SUB + rows - 1)):
-            for half in range(halves):
-                row_send[sweep, comp, way, half : half + 1, :] = coarse[buf][
-                    comp, half, line : line + 1, :
+            for tile in range(halves + 1):
+                row_send[sweep, comp, way, tile : tile + 1, :] = coarse[buf][
+                    comp, tile, line : line + 1, :
                 ]
-        start_all(coarse_message, sweep, comp, (0, 1, 4, 5, 6, 7))
-        turned = jnp.where(
-            low, coarse[buf][comp, 0, inner, :], coarse[buf][comp, halves - 1, inner, :]
-        ).T
-        col_send[sweep, comp, 0] = turned[0:1]
-        col_send[sweep, comp, 1] = turned[LANES - 1 : LANES]
-        start_all(coarse_message, sweep, comp, (2, 3))
-
-    first_row = lax.broadcasted_iota(jnp.int32, (1, LANES), 1) < HALF
+            message(
+                way,
+                row_send.at[sweep, comp, way],
+                row_recv.at[sweep, comp, 1 - way],
+                halo_send,
+                halo_recv.at[sweep, comp],
+            )
 
     def take_coarse(sweep, comp):
         buf = sweep % 2
-        wait_all(halo_recv.at[sweep, comp], halves, rows // LANES, halves)
+        for count_x, at_x in sides_x:
+
+            @pl.when(at_x)
+            def _():
+                units = row_send.shape[3] * count_x
+                wait_bytes(tally.at[pl.ds(0, units)], halo_recv.at[sweep, comp])
+
         for way, line in enumerate((SUB - 1, SUB + rows)):
-            for half in range(halves):
-                coarse[buf][comp, half, line : line + 1, :] = row_recv[
-                    sweep, comp, way, half : half + 1, :
+            for tile in range(halves + 1):
+                coarse[buf][comp, tile, line : line + 1, :] = row_recv[
+                    sweep, comp, way, tile : tile + 1, :
                 ]
-        coarse_halo[comp, inner, :] = spread_rows(
-            col_recv[sweep, comp, 0], col_recv[sweep, comp, 1]
-        )
-        for (before, after), line in zip(((0, 2), (3, 1)), (SUB - 1, SUB + rows)):
-            left = corner_recv[sweep, comp, before, halves - 1 : halves, :]
-            right = corner_recv[sweep, comp, after, 0:1, :]
-            coarse_halo[comp, line : line + 1, :] = jnp.where(
-                first_row, pltpu.roll(left, 1, 1), pltpu.roll(right, LANES - 1, 1)
-            )
 
     zero = jnp.zeros((SUB, LANES), jnp.float32)
 
@@ -468,39 +537,44 @@
             totals = list(totals)
             lines = plain(block)
             out = []
-            halo = coarse_halo[comp, rows_of(block), :]
-            own = [coarse[buf][comp, half, rows_of(block), :] for half in range(halves)]
-            lefts, rights = from_left(own, halo), from_right(own, halo)
-            for half in range(halves):
-                columns = slice(half * LANES, (half + 1) * LANES)
+            ring = [coarse[buf][comp, tile, rows_of(block), :] for tile in range(halves + 1)]
+            lefts, rights = from_left(ring), from_right(ring)
+            for tile in range(halves if last else halves + 1):
+                columns = slice(tile * LANES, (tile + 1) * LANES)
                 near = (
-                    coarse[buf][comp, half, rows_of(block, 1), :]
-                    + coarse[buf][comp, half, rows_of(block, -1), :]
-                    + rights[half]
-                    + lefts[half]
+                    coarse[buf][comp, tile, rows_of(block, 1), :]
+                    + coarse[buf][comp, tile, rows_of(block, -1), :]
+                    + rights[tile]
+                    + lefts[tile]
                 )
-                below = (
-                    fine[buf][comp, 0, 0, half, rows_of(block), :]
-                    + fine[buf][comp, 1, 0, half, rows_of(block), :]
-                    + fine[buf][comp, 0, 1, half, rows_of(block), :]
-                    + fine[buf][comp, 1, 1, half, rows_of(block), :]
-                )
-                res = (
-                    patch_known[comp, lines, columns]
-                    + 0.25 * near
-                    + 0.125 * below
-                    - patch_mu[lines, columns] * own[half]
-                )
-                totals[half % 2] = totals[half % 2] + res * res
-                out.append((half, own[half] + res * patch_inverse[lines, columns]))
-            for half, new in out:
+                if tile < halves:
+                    below = (
+                        fine[buf][comp, 0, 0, tile, rows_of(block), :]
+                        + fine[buf][comp, 1, 0, tile, rows_of(block), :]
+                        + fine[buf][comp, 0, 1, tile, rows_of(block), :]
+                        + fine[buf][comp, 1, 1, tile, rows_of(block), :]
+                    )
+                    given = patch_known[comp, lines, columns]
+                    scale, reciprocal = patch_mu[lines, columns], patch_inverse[lines, columns]
+                else:
+                    below = roll_lanes(fine_halo[comp, lines, :], -QUARTER)
+                    given = strip_known[comp, lines, :]
+                    scale, reciprocal = strip_mu[lines, :], strip_inverse[lines, :]
+                res = given + 0.25 * near + 0.125 * below - scale * ring[tile]
+                new = ring[tile] + res * reciprocal
+                if tile < halves:
+                    totals[tile % 2] = totals[tile % 2] + res * res
+                else:
+                    new = jnp.where(valid, new, 0.0)
+                out.append((tile, new))
+            for tile, new in out:
                 if last:
-                    patch_out[comp, lines, half * LANES : (half + 1) * LANES] = new
+                    patch_out[comp, lines, tile * LANES : (tile + 1) * LANES] = new
                 else:
-                    coarse[1 - buf][comp, half, rows_of(block), :] = new
+                    coarse[1 - buf][comp, tile, rows_of(block), :] = new
             return tuple(totals)
 
-        return sum(lax.fori_loop(0, blocks, body, (zero,) * 2, unroll=4))
+        return sum(lax.fori_loop(0, blocks, body, (zero,) * 2, unroll=COARSE_UNROLL))
 
     def fine_pass(sweep, comp):
         buf = sweep % 2
@@ -508,24 +582,21 @@
         def body(block, totals):
             totals = list(totals)
             out = []
-            mid = [coarse[buf][comp, half, rows_of(block), :] for half in range(halves)]
-            mid_halo = coarse_halo[comp, rows_of(block), :]
+            mid = [coarse[buf][comp, tile, rows_of(block), :] for tile in range(halves + 1)]
             fine_edges = fine_halo[comp, plain(block), :]
             for parity in range(2):
                 shift = 1 if parity else -1
-                far_halo = coarse_halo[comp, rows_of(block, shift), :]
                 line = [
-                    0.75 * mid[half] + 0.25 * coarse[buf][comp, half, rows_of(block, shift), :]
-                    for half in range(halves)
+                    0.75 * mid[tile] + 0.25 * coarse[buf][comp, tile, rows_of(block, shift), :]
+                    for tile in range(halves + 1)
                 ]
-                line_halo = 0.75 * mid_halo + 0.25 * far_halo
-                line_left, line_right = from_left(line, line_halo), from_right(line, line_halo)
+                line_left, line_right = from_left(line), from_right(line)
                 edge = roll_lanes(fine_edges, HALF) if parity else fine_edges
                 evens, odds = (
                     [fine[buf][comp, parity, side, half, rows_of(block), :] for half in range(halves)]
                     for side in range(2)
                 )
-                before, after = from_left(odds, edge), from_right(evens, edge)
+                before, after = beside_left(odds, edge), beside_right(evens, edge)
                 for half in range(halves):
                     for side in range(2):
                         own = odds[half] if side else evens[half]
@@ -552,7 +623,7 @@
                 fine[1 - buf][comp, parity, side, half, rows_of(block), :] = new
             return tuple(totals)
 
-        return sum(lax.fori_loop(0, blocks, body, (zero,) * 4, unroll=2))
+        return sum(lax.fori_loop(0, blocks, body, (zero,) * 4, unroll=FINE_UNROLL))
 
     def back_rows(owner):
         return pl.ds(pl.multiple_of(owner * own_rows, SUB), own_rows)
@@ -595,7 +666,7 @@
                 fine_out[tile, comp, at, :] = cells
             return carry
 
-        lax.fori_loop(0, blocks, body, 0, unroll=4)
+        lax.fori_loop(0, blocks, body, 0, unroll=SPLIT_UNROLL)
 
     totals = [zero] * ITERS
 
@@ -616,46 +687,18 @@
         on_fine(0, comp)
         send_fine(1, comp)
 
-    send_moves(START)
-    wait_bytes(raw_start, load_sem.at[0])
-    for comp in range(comps):
-        send_fine_cols(0, comp)
-    open_moves()
-    for comp in range(comps):
-        split_start(comp)
-        send_fine_rows(0, comp)
-    wait_bytes(raw_mu, load_sem.at[1])
-    lax.fori_loop(0, blocks, split_mu, 0, unroll=2)
-    wait_bytes(raw_known, load_sem.at[2])
-    place(0)
-    next_moves(0)
-    split_known(0)
-    place(1)
-    next_moves(1)
-    first_fine(0)
-    split_known(1)
-    place(2)
-    next_moves(2)
-    first_fine(1)
-    split_known(2)
-    first_fine(2)
-    wait_moves(MU)
-    next_moves(MU)
-    place_mu()
-
     def first_coarse(comp):
         wait_moves(KNOWN + comp)
         on_coarse(0, comp)
         send_coarse(1, comp)
-        next_moves(KNOWN + comp)
 
     def second_coarse(comp):
+        take_fine(1, comp)
         take_coarse(1, comp)
         on_coarse(1, comp)
         send_coarse(2, comp)
 
     def second_fine(comp):
-        take_fine(1, comp)
         on_fine(1, comp)
         send_fine(2, comp)
 
@@ -673,23 +716,55 @@
     def gather_sum(sums, sweep):
         return jnp.where(one_lane == sweep, jnp.sum(totals[sweep]), sums)
 
+    send_moves(START)
+    send_strips()
+    wait_bytes(raw_start, load_sem.at[0])
+    for comp in range(comps):
+        send_fine_cols(0, comp)
+    send_moves(START + 1)
+    send_moves(START + 2)
+    send_moves(MU)
+    send_moves(KNOWN)
+    send_moves(KNOWN + 1)
+    send_moves(KNOWN + 2)
+    split_start(0)
+    send_fine_rows(0, 0)
+    split_start(1)
+    send_fine_rows(0, 1)
+    split_start(2)
+    send_fine_rows(0, 2)
+    wait_bytes(raw_mu, load_sem.at[1])
+    lax.fori_loop(0, blocks, split_mu, 0, unroll=MU_UNROLL)
+    wait_bytes(raw_known, load_sem.at[2])
+    split_known(0)
+    split_known(1)
+    split_known(2)
+    take_strips()
+    place(0)
+    first_fine(0)
+    place(1)
+    first_fine(1)
+    place(2)
+    first_fine(2)
+    wait_moves(MU)
+    place_mu()
     first_coarse(0)
     first_coarse(1)
+    first_coarse(2)
     second_coarse(0)
     second_fine(0)
-    first_coarse(2)
     second_coarse(1)
+    second_fine(1)
     last_coarse(0)
-    second_fine(1)
     second_coarse(2)
+    second_fine(2)
     last_coarse(1)
-    second_fine(2)
+    last_coarse(2)
     last_fine(0)
-    last_coarse(2)
+    last_fine(1)
     sums = jnp.zeros((1, LANES), jnp.float32)
     for sweep in range(ITERS - 1):
         sums = gather_sum(sums, sweep)
-    last_fine(1)
     last_fine(2)
     norm_all[me] = gather_sum(sums, ITERS - 1)
     each_device(
@@ -702,20 +777,21 @@
             device_id_type=MESH,
         ).start()
     )
-    for comp in range(comps):
-        weave(comp)
-
-    for direction in range(8):
-        way = direction % 2 if direction < 4 else 0 if DIRECTIONS[direction][0] < 0 else 1
+    weave(0)
+    weave(1)
+    weave(2)
+
+    for direction in range(4):
+        way = direction % 2
 
         @pl.when(inside(direction))
         def _():
-            sent = (col_send if direction in (2, 3) else row_send).at[:, :, way]
-            wait_sent(sent, halo_send.at[direction])
-            if direction < 4:
-                sent = (fine_col_send if direction > 1 else fine_row_send).at[:, :, way]
-                wait_sent(sent, fine_send.at[direction])
-
+            sent = (fine_row_send if direction < 2 else fine_col_send).at[:, :, way]
+            wait_sent(sent, fine_send.at[direction])
+            if direction < 2:
+                wait_sent(row_send.at[:, :, way], halo_send.at[direction])
+
+    wait_sent(strip_send.at[pl.ds(0, n_gy - 1)], edge_send.at[0])
     others = pl.ds(0, rows - own_rows)
     wait_sent(patch_start.at[:, others, :], move_send.at[0])
     wait_sent(patch_mu.at[others, :], move_send.at[1])
@@ -754,6 +830,7 @@
     halves = width // LANES
     tiles = 2 * halves
     padded = rows + 2 * SUB
+    row_pad = 1 << halves.bit_length()
     cells_total = 3.0 * (fine_mu.size + coarse_mu.size) * n_gx * n_gy
     f32 = jnp.float32
     dma = pltpu.SemaphoreType.DMA
@@ -782,29 +859,33 @@
             pltpu.VMEM((comps, rows, width), f32),
             pltpu.VMEM((rows, width), f32),
             pltpu.VMEM((rows, width), f32),
-            pltpu.VMEM((comps, halves, padded, LANES), f32),
-            pltpu.VMEM((comps, halves, padded, LANES), f32),
+            pltpu.VMEM((comps, halves + 1, padded, LANES), f32),
+            pltpu.VMEM((comps, halves + 1, padded, LANES), f32),
             pltpu.VMEM((comps, rows, width), f32),
             pltpu.VMEM((ITERS, comps, 2, tiles, LANES), f32),
             pltpu.VMEM((ITERS, comps, 2, tiles, LANES), f32),
-            pltpu.VMEM((ITERS, comps, 2, 2, rows), f32),
-            pltpu.VMEM((ITERS, comps, 2, 2, rows), f32),
-            pltpu.VMEM((ITERS, comps, 2, halves, LANES), f32),
-            pltpu.VMEM((ITERS, comps, 2, halves, LANES), f32),
-            pltpu.VMEM((ITERS, comps, 2, 1, rows), f32),
-            pltpu.VMEM((ITERS, comps, 2, 1, rows), f32),
-            pltpu.VMEM((ITERS, comps, 4, halves, LANES), f32),
+            pltpu.VMEM((ITERS, comps, 2, 4, rows), f32),
+            pltpu.VMEM((ITERS, comps, 2, 4, rows), f32),
+            pltpu.VMEM((ITERS, comps, 2, row_pad, LANES), f32),
+            pltpu.VMEM((ITERS, comps, 2, row_pad, LANES), f32),
             pltpu.VMEM((comps, rows, LANES), f32),
-            pltpu.VMEM((comps, padded, LANES), f32),
+            pltpu.VMEM((2 * comps + 1,) + coarse_mu.shape, f32),
+            pltpu.VMEM((n_gy, SUB, LANES), f32),
+            pltpu.VMEM((n_gy, SUB, LANES), f32),
+            pltpu.VMEM((comps, rows, LANES), f32),
+            pltpu.VMEM((rows, LANES), f32),
+            pltpu.VMEM((rows, LANES), f32),
             pltpu.VMEM((n_gx * n_gy, 1, LANES), f32),
-            pltpu.VMEM((6 * halves + 4 * rows // LANES, 1, LANES), f32),
-            dma((3,)),
+            pltpu.VMEM((2 * tiles + 2 * row_pad + 8 * rows // LANES, 1, LANES), f32),
+            dma((4,)),
             dma((3,)),
             dma((2 * comps + 1,)),
             dma((4,)),
             dma((ITERS, comps)),
-            dma((8,)),
+            dma((2,)),
             dma((ITERS, comps)),
+            dma((1,)),
+            dma((1,)),
             dma((1,)),
             dma((1,)),
             dma((1,)),

time: 51 us -> 47 us (0.922)
  Pallas kernels: 50.2 us -> 46.2 us
    pallas_call x1, Pallas kernels: 48.4 us -> 44.4 us  [on_device(): pl.pallas_call(functools.partial(kernel, n_gx, n_gy, cells_total), out_sh...]
where the time goes in v2:
time: 47 us; the launch traced here: 46.9 us
  Pallas kernels  46.2 us (98%)
  between operations  0.64 us (1%)
    pallas_call x1, Pallas kernels, on_device(): pl.pallas_call(functools.partial(kernel, n_gx, n_gy, cells_total), out_sh...  44.4 us
    pallas_call x1, Pallas kernels, on_device(): pl.pallas_call(finish, out_shape=(jax.ShapeDtypeStruct(fine_start.shape,...  1.82 us

profile of v2, /device:TPU:0, one launch (start us, length us, event | category | flops | bytes accessed | tf_op | source)
XLA Modules:
  0.0 46.9 jit_solution(17108220100156867220)
XLA Ops:
  0.6 44.4 %shard_map.85 = (f32[4,3,256,128]{3,2,1,0:T(8,128)S(1)}, f32[3,16,2048]{2,1,0:T(8,128)S(1)}, f32[8,128]{1,0:T(8,128)S(1)}) custom-call(f32[3,256,512]{2,1,0:T(8,128)} %fine_start.1, f32[3,256,512]{2,1,0:T(8,128)} %fine_known.1, f32[256,512]{1,0:T(8,128)} %fine_mu.1, f32[3,16,2048]{2,1,0:T(8,128)} %coarse_start.1, f32[3,16,2048]{2,1,0:T(8,128)} %coarse_known.1, ...), custom_call_target="tpu_custom_call" | custom-call | tf_op jit(solution)/shard_map/pallas_call | solution.py:840
  45.0 1.8 %shard_map.86 = (f32[3,256,512]{2,1,0:T(8,128)}, f32[3,16,2048]{2,1,0:T(8,128)}, f32[3]{0:T(128)}) custom-call(f32[4,3,256,128]{3,2,1,0:T(8,128)S(1)} %get-tuple-element.6.fine_in, f32[3,16,2048]{2,1,0:T(8,128)S(1)} %get-tuple-element.7.coarse_in, f32[8,128]{1,0:T(8,128)S(1)} %get-tuple-element.8.norms_in), custom_call_target="tpu_custom_call" | custom-call | tf_op jit(solution)/shard_map/pallas_call | solution.py:900

commit v3 on v2

--- a/solution.py
+++ b/solution.py
@@ -139,6 +139,12 @@
         lambda peer: pl.semaphore_signal(barrier, inc=1, device_id=peer, device_id_type=MESH)
     )
 
+    pltpu.make_async_copy(coarse_start, own_planes.at[pl.ds(0, comps)], load_sem.at[3]).start()
+    pltpu.make_async_copy(coarse_mu, own_planes.at[comps], load_sem.at[3]).start()
+    pltpu.make_async_copy(
+        coarse_known, own_planes.at[pl.ds(comps + 1, comps)], load_sem.at[3]
+    ).start()
+
     loads = []
     for which, (source, target) in enumerate(
         ((fine_start, raw_start), (fine_mu, raw_mu), (fine_known, raw_known))
@@ -160,12 +166,6 @@
             ref, ref, sem, sem, device_id={"gy": gy}, device_id_type=MESH
         ).wait_send()
 
-    pltpu.make_async_copy(coarse_start, own_planes.at[pl.ds(0, comps)], load_sem.at[3]).start()
-    pltpu.make_async_copy(coarse_mu, own_planes.at[comps], load_sem.at[3]).start()
-    pltpu.make_async_copy(
-        coarse_known, own_planes.at[pl.ds(comps + 1, comps)], load_sem.at[3]
-    ).start()
-
     def clear(edge, ref, way):
         @pl.when(edge)
         def _():
@@ -197,13 +197,12 @@
     def plane(item, owner, place):
         columns = pl.ds(pl.multiple_of(owner * width, LANES), width)
         lines = pl.ds(pl.multiple_of(place * own_rows, SUB), own_rows)
+        source = own_planes.at[item, :, columns]
         if item == MU:
-            return coarse_mu.at[:, columns], patch_mu.at[lines, :]
-        comp = item - START if item < MU else item - KNOWN
-        source, target = (
-            (coarse_start, patch_start) if item < MU else (coarse_known, patch_known)
-        )
-        return source.at[comp, :, columns], target.at[comp, lines, :]
+            return source, patch_mu.at[lines, :]
+        if item < MU:
+            return source, patch_start.at[item - START, lines, :]
+        return source, patch_known.at[item - KNOWN, lines, :]
 
     def each_step(action):
         def body(step, carry):
@@ -211,6 +210,8 @@
             return carry
 
         lax.fori_loop(1, n_gy, body, 0)
+
+    own_columns = pl.ds(pl.multiple_of(gy * width, LANES), width)
 
     def send_moves(item):
         kind = 0 if item < MU else 1 if item == MU else 2
@@ -225,7 +226,13 @@
             ).start()
 
         each_step(send)
-        pltpu.make_async_copy(*plane(item, gy, gy), move_recv.at[item]).start()
+        if item == MU:
+            source = coarse_mu.at[:, own_columns]
+        elif item < MU:
+            source = coarse_start.at[item - START, :, own_columns]
+        else:
+            source = coarse_known.at[item - KNOWN, :, own_columns]
+        pltpu.make_async_copy(source, plane(item, gy, gy)[1], move_recv.at[item]).start()
 
     def wait_moves(item):
         if item == MU:
@@ -246,7 +253,6 @@
         return tile * share + 2 * REACH * item
 
     def send_strips():
-        wait_bytes(own_planes, load_sem.at[3])
         for owner in range(n_gy):
             cells = jnp.zeros((SUB, LANES), jnp.float32)
             for tile in range(own_tiles):
@@ -716,6 +722,7 @@
     def gather_sum(sums, sweep):
         return jnp.where(one_lane == sweep, jnp.sum(totals[sweep]), sums)
 
+    wait_bytes(own_planes, load_sem.at[3])
     send_moves(START)
     send_strips()
     wait_bytes(raw_start, load_sem.at[0])
@@ -724,9 +731,6 @@
     send_moves(START + 1)
     send_moves(START + 2)
     send_moves(MU)
-    send_moves(KNOWN)
-    send_moves(KNOWN + 1)
-    send_moves(KNOWN + 2)
     split_start(0)
     send_fine_rows(0, 0)
     split_start(1)
@@ -741,8 +745,11 @@
     split_known(2)
     take_strips()
     place(0)
+    send_moves(KNOWN)
+    send_moves(KNOWN + 1)
     first_fine(0)
     place(1)
+    send_moves(KNOWN + 2)
     first_fine(1)
     place(2)
     first_fine(2)
@@ -807,19 +814,21 @@
     wait_bytes(coarse_out.at[:, :, pl.ds(0, (n_gy - 1) * width)], back_recv.at[0])
 
 
-def finish(fine_in, coarse_in, norms_in, fine_out, coarse_out, norms_out, sems):
+def finish(fine_in, coarse_in, norms_in, fine_out, coarse_out, norms_out, held, sems):
     tiles = fine_in.shape[0]
-    copies = [pltpu.make_async_copy(coarse_in, coarse_out, sems.at[tiles])]
-    for tile in range(tiles):
-        copies.append(
-            pltpu.make_async_copy(
-                fine_in.at[tile], fine_out.at[:, :, pl.ds(tile * LANES, LANES)], sems.at[tile]
-            )
+    copies = [
+        pltpu.make_async_copy(
+            fine_in.at[tile], fine_out.at[:, :, pl.ds(tile * LANES, LANES)], sems.at[tile]
         )
+        for tile in range(tiles)
+    ]
+    copies.append(pltpu.make_async_copy(coarse_in, coarse_out, sems.at[tiles]))
     for copy in copies:
         copy.start()
     for sweep in range(ITERS):
-        norms_out[sweep] = norms_in[0, sweep]
+        held[sweep] = norms_in[0, sweep]
+    copies.append(pltpu.make_async_copy(held, norms_out, sems.at[tiles + 1]))
+    copies[-1].start()
     for copy in copies:
         copy.wait()
 
@@ -905,8 +914,8 @@
             jax.ShapeDtypeStruct((ITERS,), f32),
         ),
         in_specs=[in_vmem] * 3,
-        out_specs=(anywhere, anywhere, pl.BlockSpec(memory_space=pltpu.SMEM)),
-        scratch_shapes=[dma((tiles + 1,))],
+        out_specs=(anywhere,) * 3,
+        scratch_shapes=[pltpu.SMEM((ITERS,), f32), dma((tiles + 2,))],
         compiler_params=pltpu.CompilerParams(vmem_limit_bytes=2**20),
     )(*(pltpu.with_memory_space_constraint(result, pltpu.VMEM) for result in results))
 

time: 47 us -> 46.2 us (0.983)
  Pallas kernels: 46.2 us -> 45.4 us
    pallas_call x1, Pallas kernels: 1.82 us -> 1.33 us  [on_device(): pl.pallas_call(finish, out_shape=(jax.ShapeDtypeStruct(fine_start.shape,...]
where the time goes in v3:
time: 46.2 us; the launch traced here: 46.1 us
  Pallas kernels  45.4 us (98%)
  between operations  0.64 us (1%)
    pallas_call x1, Pallas kernels, on_device(): pl.pallas_call(functools.partial(kernel, n_gx, n_gy, cells_total), out_sh...  44.1 us
    pallas_call x1, Pallas kernels, on_device(): pl.pallas_call(finish, out_shape=(jax.ShapeDtypeStruct(fine_start.shape,...  1.33 us

profile of v3, /device:TPU:0, one launch (start us, length us, event | category | flops | bytes accessed | tf_op | source)
XLA Modules:
  0.0 46.1 jit_solution(11215700363814357781)
XLA Ops:
  0.6 44.1 %shard_map.85 = (f32[4,3,256,128]{3,2,1,0:T(8,128)S(1)}, f32[3,16,2048]{2,1,0:T(8,128)S(1)}, f32[8,128]{1,0:T(8,128)S(1)}) custom-call(f32[3,256,512]{2,1,0:T(8,128)} %fine_start.1, f32[3,256,512]{2,1,0:T(8,128)} %fine_known.1, f32[256,512]{1,0:T(8,128)} %fine_mu.1, f32[3,16,2048]{2,1,0:T(8,128)} %coarse_start.1, f32[3,16,2048]{2,1,0:T(8,128)} %coarse_known.1, ...), custom_call_target="tpu_custom_call" | custom-call | tf_op jit(solution)/shard_map/pallas_call | solution.py:849
  44.7 1.3 %shard_map.86 = (f32[3,256,512]{2,1,0:T(8,128)}, f32[3,16,2048]{2,1,0:T(8,128)}, f32[3]{0:T(128)}) custom-call(f32[4,3,256,128]{3,2,1,0:T(8,128)S(1)} %get-tuple-element.6.fine_in, f32[3,16,2048]{2,1,0:T(8,128)S(1)} %get-tuple-element.7.coarse_in, f32[8,128]{1,0:T(8,128)S(1)} %get-tuple-element.8.norms_in), custom_call_target="tpu_custom_call" | custom-call | tf_op jit(solution)/shard_map/pallas_call | solution.py:909

commit v4 on v3

--- a/solution.py
+++ b/solution.py
@@ -125,15 +125,14 @@
     lane = lane_index()
     barrier = pltpu.get_barrier_semaphore()
 
+    def wrap(at, size):
+        return jnp.where(at < size, at, at - size)
+
     def each_device(action):
-        def along_gx(dx, carry):
-            def along_gy(dy, inner_carry):
-                action({"gx": lax.rem(gx + dx, n_gx), "gy": lax.rem(gy + dy, n_gy)})
-                return inner_carry
-
-            return lax.fori_loop(jnp.where(dx == 0, 1, 0), n_gy, along_gy, carry)
-
-        lax.fori_loop(0, n_gx, along_gx, 0)
+        for dy in reversed(range(n_gy)):
+            for dx in range(n_gx):
+                if dx or dy:
+                    action({"gx": wrap(gx + dx, n_gx), "gy": wrap(gy + dy, n_gy)})
 
     each_device(
         lambda peer: pl.semaphore_signal(barrier, inc=1, device_id=peer, device_id_type=MESH)

time: 46.2 us -> 46 us (level)
  no operation moved by 1% of the time
where the time goes in v4:
time: 46 us; the launch traced here: 45.8 us
  Pallas kernels  45.2 us (98%)
  between operations  0.64 us (1%)
    pallas_call x1, Pallas kernels, on_device(): pl.pallas_call(functools.partial(kernel, n_gx, n_gy, cells_total), out_sh...  43.9 us
    pallas_call x1, Pallas kernels, on_device(): pl.pallas_call(finish, out_shape=(jax.ShapeDtypeStruct(fine_start.shape,...  1.33 us

profile of v4, /device:TPU:0, one launch (start us, length us, event | category | flops | bytes accessed | tf_op | source)
XLA Modules:
  0.0 45.8 jit_solution(15484976960111967204)
XLA Ops:
  0.6 43.9 %shard_map.85 = (f32[4,3,256,128]{3,2,1,0:T(8,128)S(1)}, f32[3,16,2048]{2,1,0:T(8,128)S(1)}, f32[8,128]{1,0:T(8,128)S(1)}) custom-call(f32[3,256,512]{2,1,0:T(8,128)} %fine_start.1, f32[3,256,512]{2,1,0:T(8,128)} %fine_known.1, f32[256,512]{1,0:T(8,128)} %fine_mu.1, f32[3,16,2048]{2,1,0:T(8,128)} %coarse_start.1, f32[3,16,2048]{2,1,0:T(8,128)} %coarse_known.1, ...), custom_call_target="tpu_custom_call" | custom-call | tf_op jit(solution)/shard_map/pallas_call | solution.py:848
  44.5 1.3 %shard_map.86 = (f32[3,256,512]{2,1,0:T(8,128)}, f32[3,16,2048]{2,1,0:T(8,128)}, f32[3]{0:T(128)}) custom-call(f32[4,3,256,128]{3,2,1,0:T(8,128)S(1)} %get-tuple-element.6.fine_in, f32[3,16,2048]{2,1,0:T(8,128)S(1)} %get-tuple-element.7.coarse_in, f32[8,128]{1,0:T(8,128)S(1)} %get-tuple-element.8.norms_in), custom_call_target="tpu_custom_call" | custom-call | tf_op jit(solution)/shard_map/pallas_call | solution.py:908
